TPU v7x, 32 devices: a whole 2x2x4 slice. The times are simulated.
32 devices in a mesh: dp: 2 (over x), sp: 4 (over z), tp: 4 (over y, core).
Axes of the slice: x: 2, y: 2, z: 4, core: 2. Of those that a mesh axis runs over, the one named last changes fastest.
Arguments:
- x: bfloat16 [8192, 4096], P(('dp', 'sp', 'tp')), parts along dimension 0
- segment_ids: int32 [8192], P(('dp', 'sp', 'tp')), parts along dimension 0
- positions: int32 [8192], P(('dp', 'sp', 'tp')), parts along dimension 0
- g_attn: bfloat16 [2, 4096], replicated
- w_q: bfloat16 [2, 4096, 32, 128], P(None, None, 'tp')
- w_k: bfloat16 [2, 4096, 8, 128], replicated
- w_v: bfloat16 [2, 4096, 8, 128], replicated
- w_o: bfloat16 [2, 32, 128, 4096], P(None, 'tp')
- g_mlp: bfloat16 [2, 4096], replicated
- w_gate: bfloat16 [2, 4096, 14336], P(None, None, 'tp')
- w_up: bfloat16 [2, 4096, 14336], P(None, None, 'tp')
- w_down: bfloat16 [2, 14336, 4096], P(None, 'tp')
Outputs:
- output: bfloat16 [8192, 4096], P(('dp', 'sp', 'tp')), parts along dimension 0
There are 2 independent parts. A program takes and returns all parts, laid end to end along the dimension named above; an argument that names none is the same for every part.
All inputs are finite; a program needn't handle non-finite values.
Results may differ from a plain program's by a relative error of at most 0.0180036.
Values are sent between devices in bfloat16 or wider.
A program may use at most 1 GiB of HBM per device.

v0:
```python
import jax
import jax.numpy as jnp
from jax import lax
from jax.sharding import PartitionSpec as P

EPS = 1e-6
ROPE_BASE = 10000.0
WINDOW = 1024
SCORE_ROWS = 256


def rms_norm(x, gain):
    x_wide = x.astype(jnp.float32)
    inv_rms = lax.rsqrt(jnp.mean(x_wide * x_wide, axis=-1, keepdims=True) + EPS)
    return (x_wide * inv_rms * gain.astype(jnp.float32)).astype(jnp.bfloat16)


def rope_tables(positions, head_dim):
    half_width = head_dim // 2
    inv_freq = ROPE_BASE ** (-jnp.arange(half_width, dtype=jnp.float32) / half_width)
    angles = positions.astype(jnp.float32)[:, None] * inv_freq[None, :]
    return jnp.cos(angles)[:, None, :], jnp.sin(angles)[:, None, :]


def rope(t, cos_tab, sin_tab):
    half_width = t.shape[-1] // 2
    t_wide = t.astype(jnp.float32)
    lower_half = t_wide[..., :half_width]
    upper_half = t_wide[..., half_width:]
    return jnp.concatenate([lower_half * cos_tab - upper_half * sin_tab, upper_half * cos_tab + lower_half * sin_tab], axis=-1).astype(jnp.bfloat16)


def attend(q, k_all, v_all, seg_q, seg_all, q_offset, windowed):
    q_rows, kv_count, group_size, head_dim = q.shape
    total = k_all.shape[0]
    block_rows = min(q_rows, max(SCORE_ROWS // (kv_count * group_size), 8))
    blocks = q_rows // block_rows
    key_span = min(block_rows + WINDOW, total) if windowed else total
    q_blocks = q.reshape(blocks, block_rows, kv_count, group_size, head_dim)
    seg_blocks = seg_q.reshape(blocks, block_rows)

    def one_block(block_args):
        q_blk, seg_blk, block_idx = block_args
        q_start = q_offset + block_idx * block_rows
        k_start = jnp.clip(q_start + block_rows - key_span, 0, total - key_span)
        k_blk = lax.dynamic_slice_in_dim(k_all, k_start, key_span, 0)
        v_blk = lax.dynamic_slice_in_dim(v_all, k_start, key_span, 0)
        seg_k = lax.dynamic_slice_in_dim(seg_all, k_start, key_span, 0)
        q_pos = q_start + jnp.arange(block_rows)
        k_pos = k_start + jnp.arange(key_span)
        allowed = (k_pos[None, :] <= q_pos[:, None]) & (seg_k[None, :] == seg_blk[:, None])
        if windowed:
            allowed = allowed & (q_pos[:, None] - k_pos[None, :] < WINDOW)
        scores = jnp.einsum("qgrd,kgd->qgrk", q_blk, k_blk, preferred_element_type=jnp.float32) * head_dim ** -0.5
        scores = jnp.where(allowed[:, None, None, :], scores, -1e30)
        attn_probs = jax.nn.softmax(scores, axis=-1).astype(jnp.bfloat16)
        return jnp.einsum("qgrk,kgd->qgrd", attn_probs, v_blk, preferred_element_type=jnp.float32).astype(jnp.bfloat16)

    out_blocks = lax.map(one_block, (q_blocks, seg_blocks, jnp.arange(blocks)))
    return out_blocks.reshape(q_rows, kv_count * group_size * head_dim)


def matmul(rows_in, weight):
    return jnp.dot(rows_in, weight, preferred_element_type=jnp.float32)


def solution(mesh):
    tp_size = mesh.shape["tp"]
    row_spec = P(("dp", "sp", "tp"), None)
    id_spec = P(("dp", "sp", "tp"))
    whole = P()
    in_specs = (row_spec, id_spec, id_spec, whole, P(None, None, "tp", None), whole, whole, P(None, "tp", None, None), whole, P(None, None, "tp"), P(None, None, "tp"), P(None, "tp", None))

    def local_fn(x, segment_ids, positions, g_attn, w_q, w_k, w_v, w_o, g_mlp, w_gate, w_up, w_down):
        sp_idx = lax.axis_index("sp")
        tp_idx = lax.axis_index("tp")
        layers, model, heads_loc, head_dim = w_q.shape
        kv_heads = w_k.shape[2]
        kv_loc = max(kv_heads // tp_size, 1)
        group_size = heads_loc // kv_loc
        kv_start = tp_idx * kv_heads // tp_size
        seg_all = lax.all_gather(segment_ids, ("sp", "tp"), tiled=True)
        pos_shard = lax.all_gather(positions, "tp", tiled=True)
        shard_rows = pos_shard.shape[0]
        q_offset = sp_idx * shard_rows
        seg_q = lax.dynamic_slice_in_dim(seg_all, q_offset, shard_rows, 0)
        cos_tab, sin_tab = rope_tables(pos_shard, head_dim)
        for layer in range(layers):
            normed = lax.all_gather(rms_norm(x, g_attn[layer]), "tp", tiled=True)
            w_k_loc = lax.dynamic_slice_in_dim(w_k[layer], kv_start, kv_loc, 1).reshape(model, kv_loc * head_dim)
            w_v_loc = lax.dynamic_slice_in_dim(w_v[layer], kv_start, kv_loc, 1).reshape(model, kv_loc * head_dim)
            q = matmul(normed, w_q[layer].reshape(model, heads_loc * head_dim)).astype(jnp.bfloat16)
            k = matmul(normed, w_k_loc).astype(jnp.bfloat16)
            v = matmul(normed, w_v_loc).astype(jnp.bfloat16)
            q = rope(q.reshape(shard_rows, heads_loc, head_dim), cos_tab, sin_tab).reshape(shard_rows, kv_loc, group_size, head_dim)
            k = rope(k.reshape(shard_rows, kv_loc, head_dim), cos_tab, sin_tab)
            k_all = lax.all_gather(k, "sp", tiled=True)
            v_all = lax.all_gather(v.reshape(shard_rows, kv_loc, head_dim), "sp", tiled=True)
            mixed = attend(q, k_all, v_all, seg_q, seg_all, q_offset, layer % 2 == 0)
            part_sum = matmul(mixed, w_o[layer].reshape(heads_loc * head_dim, model)).astype(jnp.bfloat16)
            attn_out = lax.psum_scatter(part_sum, "tp", scatter_dimension=0, tiled=True)
            hidden = (x.astype(jnp.float32) + attn_out.astype(jnp.float32)).astype(jnp.bfloat16)
            normed = lax.all_gather(rms_norm(hidden, g_mlp[layer]), "tp", tiled=True)
            activation = (jax.nn.silu(matmul(normed, w_gate[layer])) * matmul(normed, w_up[layer])).astype(jnp.bfloat16)
            part_sum = matmul(activation, w_down[layer]).astype(jnp.bfloat16)
            mlp_out = lax.psum_scatter(part_sum, "tp", scatter_dimension=0, tiled=True)
            x = (hidden.astype(jnp.float32) + mlp_out.astype(jnp.float32)).astype(jnp.bfloat16)
        return x

    return jax.shard_map(local_fn, mesh=mesh, in_specs=in_specs, out_specs=row_spec, check_vma=False)
```

profile of v0, /device:TPU:0, one launch (start us, length us, event | category | flops | bytes accessed | tf_op | source)
XLA Modules:
  0.0 1569.2 jit_solution(2711064970988325599)
XLA Ops:
  13.7 6.5 fusion.133
  20.2 5.2 constant_dynamic-slice_fusion.3
  29.3 6.1 all-gather.1
  37.3 37.7 %all-gather.11.cloned.1.call-done = bf16[1024,4096]{1,0:T(8,128)(2,1)} async-done(((bf16[256,4096]{1,0:T(8,128)(2,1)}), bf16[1024,4096]{1,0:T(8,128)(2,1)}) %all-gather.11.cloned.1.call-update) | async-done | bytes 8388624 | tf_op jit(solution)/shard_map/all_gather | solution.py:89
  75.1 6.3 convolution_convert_fusion.5
  85.6 6.5 fusion.132
  92.1 5.2 constant_dynamic-slice_fusion.2
  101.2 12.0 fusion.131
  113.2 5.7 convolution_convert_fusion.6
  120.0 11.3 fusion.134
  131.4 20.5 %all-gather = s32[16,1,256]{2,1,0:T(1,128)S(1)} all-gather(s32[1,1,256]{2,1,0:T(1,128)S(1)} %bitcast.234), channel_id=1, replica_groups=mesh['dp'=2,'sp'=4,'tp'=4] {'sp','tp'}, dimensions={0}, use_global_device_ids=true | all-gather | bytes 17408 | tf_op jit(solution)/shard_map/all_gather | solution.py:82
  152.0 13.8 fusion.114
  182.1 191.2 %while.28 = (s32[]{:T(128)}, bf16[32,32,2,4,128]{4,3,2,1,0:T(4,128)(2,1)S(1)}, s32[32]{0:T(128)S(1)}, s32[]{:T(128)}, bf16[4096,2,128]{2,0,1:T(8,128)(2,1)}, /*i...) while((s32[]{:T(128)}, ...), condition=%wide.region_4.5_spmd, body=%wide.region_1.4_spmd.sunk | while | flops 140271712 | bytes 3696617 | solution.py:59
  376.1 15.1 convolution_convert_fusion.2
  392.6 66.7 %reduce-scatter.5.cloned.1.call-done = bf16[256,4096]{1,0:T(8,128)(2,1)} async-done(((bf16[1024,4096]{1,0:T(8,128)(2,1)}), bf16[256,4096]{1,0:T(8,128)(2,1)}) %reduce-scatter.5.cloned.1.call-update) | async-done | bytes 2097168 | tf_op jit(solution)/shard_map/reduce_scatter | solution.py:101
  464.3 58.6 %all-gather.17.cloned.1.call-done = bf16[1024,4096]{1,0:T(8,128)(2,1)} async-done(((bf16[256,4096]{1,0:T(8,128)(2,1)}), bf16[1024,4096]{1,0:T(8,128)(2,1)}) %all-gather.17.cloned.1.call-update) | async-done | bytes 8388624 | tf_op jit(solution)/shard_map/all_gather | solution.py:103
  522.9 37.4 %fusion.74 = f32[1024,3584]{1,0:T(8,128)S(1)} fusion(bf16[1024,4096]{1,0:T(8,128)(2,1)} %all-gather.17.cloned.1.call-done, bf16[2,4096,3584]{2,1,0:T(8,128)(2,1)} %param.25), kind=kOutput, calls=%fused_computation.67 | convolution fusion | flops 30064771072 | bytes 52428800 | tf_op jit(solution)/shard_map/dot_general | solution.py:64
  560.3 36.3 %multiply_convert_fusion.1 = bf16[1024,3584]{1,0:T(8,128)(2,1)} fusion(f32[1024,3584]{1,0:T(8,128)S(1)} %fusion.74, bf16[1024,4096]{1,0:T(8,128)(2,1)S(1)} %copy-done.22, bf16[2,4096,3584]{2,1,0:T(8,128)(2,1)} %param.26), kind=kOutput, calls=%fused_computation.76 | convolution fusion | flops 30086791168 | bytes 59768832 | tf_op jit(solution)/shard_map/dot_general | solution.py:64
  596.6 37.5 %fusion.92 = bf16[1024,4096]{1,0:T(8,128)(2,1)} fusion(bf16[1024,3584]{1,0:T(8,128)(2,1)} %multiply_convert_fusion.1, bf16[2,3584,4096]{2,1,0:T(8,128)(2,1)} %param.27), kind=kOutput, calls=%fused_computation.83 | convolution fusion | flops 30068965376 | bytes 45088768 | tf_op jit(solution)/shard_map/dot_general | solution.py:64
  634.3 70.6 %reduce-scatter.7.cloned.1.call-done = bf16[256,4096]{1,0:T(8,128)(2,1)} async-done(((bf16[1024,4096]{1,0:T(8,128)(2,1)}), bf16[256,4096]{1,0:T(8,128)(2,1)}) %reduce-scatter.7.cloned.1.call-update) | async-done | bytes 2097168 | tf_op jit(solution)/shard_map/reduce_scatter | solution.py:106
  715.7 54.8 %all-gather.19.cloned.1.call-done = bf16[1024,4096]{1,0:T(8,128)(2,1)} async-done(((bf16[256,4096]{1,0:T(8,128)(2,1)}), bf16[1024,4096]{1,0:T(8,128)(2,1)}) %all-gather.19.cloned.1.call-update) | async-done | bytes 8388624 | tf_op jit(solution)/shard_map/all_gather | solution.py:89
  770.5 6.5 convolution_convert_fusion.3
  781.8 6.3 convolution_convert_fusion.4
  792.7 13.8 fusion.117
  823.4 45.9 %all-gather.21.cloned.1.call-done = bf16[4096,2,128]{2,0,1:T(8,128)(2,1)} async-done(((bf16[1024,2,128]{2,0,1:T(8,128)(2,1)}), bf16[4096,2,128]{2,0,1:T(8,128)(2,1)}) %all-gather.21.cloned.1.call-update) | async-done | bytes 2097168 | tf_op jit(solution)/shard_map/all_gather | solution.py:97
  870.3 354.4 %while.29 = (s32[]{:T(128)}, bf16[32,32,2,4,128]{4,3,2,1,0:T(4,128)(2,1)S(1)}, s32[32]{0:T(128)S(1)}, s32[]{:T(128)}, s32[4096]{0:T(1024)S(1)}, /*index=5*/s32[3...) while((s32[]{:T(128)}, ...), condition=%wide.region_12.13_spmd, body=%wide.region_9.12_spmd.sunk | while | flops 543596544 | bytes 13159765 | solution.py:59
  883.6 5.1 fusion.183
  927.9 5.1 fusion.183
  950.0 5.1 fusion.183
  983.3 5.1 fusion.183
  994.4 5.1 fusion.183
  1016.5 5.1 fusion.183
  1027.6 5.1 fusion.183
  1049.8 5.1 fusion.183
  1060.8 5.1 fusion.183
  1071.9 5.1 fusion.183
  1083.0 5.1 fusion.183
  1094.1 5.1 fusion.183
  1105.1 5.1 fusion.183
  1116.2 5.1 fusion.183
  1127.3 5.1 fusion.183
  1227.4 14.8 convolution_convert_fusion.1
  1242.3 69.8 %reduce-scatter.9.cloned.1.call-done = bf16[256,4096]{1,0:T(8,128)(2,1)} async-done(((bf16[1024,4096]{1,0:T(8,128)(2,1)}), bf16[256,4096]{1,0:T(8,128)(2,1)}) %reduce-scatter.9.cloned.1.call-update) | async-done | bytes 2097168 | tf_op jit(solution)/shard_map/reduce_scatter | solution.py:101
  1317.0 58.6 %all-gather.25.cloned.1.call-done = bf16[1024,4096]{1,0:T(8,128)(2,1)} async-done(((bf16[256,4096]{1,0:T(8,128)(2,1)}), bf16[1024,4096]{1,0:T(8,128)(2,1)}) %all-gather.25.cloned.1.call-update) | async-done | bytes 8388624 | tf_op jit(solution)/shard_map/all_gather | solution.py:103
  1375.6 37.1 %fusion.68 = f32[1024,3584]{1,0:T(8,128)S(1)} fusion(bf16[1024,4096]{1,0:T(8,128)(2,1)} %all-gather.25.cloned.1.call-done, bf16[2,4096,3584]{2,1,0:T(8,128)(2,1)} %param.25), kind=kOutput, calls=%fused_computation.61 | convolution fusion | flops 30064771072 | bytes 52428800 | tf_op jit(solution)/shard_map/dot_general | solution.py:64
  1412.8 36.3 %multiply_convert_fusion = bf16[1024,3584]{1,0:T(8,128)(2,1)} fusion(f32[1024,3584]{1,0:T(8,128)S(1)} %fusion.68, bf16[1024,4096]{1,0:T(8,128)(2,1)S(1)} %copy-done.23, bf16[2,4096,3584]{2,1,0:T(8,128)(2,1)} %param.26), kind=kOutput, calls=%fused_computation.75 | convolution fusion | flops 30086791168 | bytes 59768832 | tf_op jit(solution)/shard_map/dot_general | solution.py:64
  1449.1 37.5 %fusion.95 = bf16[1024,4096]{1,0:T(8,128)(2,1)} fusion(bf16[1024,3584]{1,0:T(8,128)(2,1)} %multiply_convert_fusion, bf16[2,3584,4096]{2,1,0:T(8,128)(2,1)} %param.27), kind=kOutput, calls=%fused_computation.84 | convolution fusion | flops 30068965376 | bytes 45088768 | tf_op jit(solution)/shard_map/dot_general | solution.py:64
  1486.7 70.8 %reduce-scatter.11.cloned.1.call-done = bf16[256,4096]{1,0:T(8,128)(2,1)} async-done(((bf16[1024,4096]{1,0:T(8,128)(2,1)}), bf16[256,4096]{1,0:T(8,128)(2,1)}) %reduce-scatter.11.cloned.1.call-update) | async-done | bytes 2097168 | tf_op jit(solution)/shard_map/reduce_scatter | solution.py:106
  (656 shorter events, 521.2 us)
Async XLA Ops:
  6.5 68.5 %all-gather.11.cloned.1.call-start = ((), (), s32[]{:S(2)}) async-start(), calls=%async_computation.4 | async-start | bytes 10485760 | tf_op jit(solution)/shard_map/all_gather | solution.py:89
  13.6 167.6 %all-gather.15.cloned.1.call-start = ((), (), s32[]{:S(2)}) async-start(), calls=%async_computation.6 | async-start | bytes 2621440 | tf_op jit(solution)/shard_map/all_gather | solution.py:97
  25.4 3.9 copy-start.20
  37.3 136.8 %copy-start.7 = (f32[1024,64]{1,0:T(8,128)}, f32[1024,64]{1,0:T(8,128)S(1)}, u32[]{:S(2)}) copy-start(f32[1024,64]{1,0:T(8,128)S(1)} %get-tuple-element.471) | copy-start | bytes 786436
  37.3 136.8 %copy-start.9 = (f32[1024,64]{1,0:T(8,128)}, f32[1024,64]{1,0:T(8,128)S(1)}, u32[]{:S(2)}) copy-start(f32[1024,64]{1,0:T(8,128)S(1)} %get-tuple-element.472) | copy-start | bytes 786436
  85.4 95.8 %all-gather.13.cloned.1.call-start = ((), (), s32[]{:S(2)}) async-start(), calls=%async_computation.5 | async-start | bytes 2621440 | tf_op jit(solution)/shard_map/all_gather | solution.py:98
  101.2 12.0 copy-start.13
  120.0 11.4 copy-start.21
  120.0 339.3 %reduce-scatter.5.cloned.1.call-start = ((), (), s32[]{:S(2)}) async-start(), calls=%async_computation.7 | async-start | bytes 10485760 | tf_op jit(solution)/shard_map/reduce_scatter | solution.py:101
  373.4 17.9 %copy-start.14 = (s32[4096]{0:T(1024)}, s32[4096]{0:T(1024)S(1)}, u32[]{:S(2)}) copy-start(s32[4096]{0:T(1024)S(1)} %get-tuple-element.716) | copy-start | bytes 49156
  373.4 17.9 %copy-start.19 = (s32[32,32]{1,0:T(8,128)}, s32[32,32]{1,0:T(8,128)S(1)}, u32[]{:S(2)}) copy-start(s32[32,32]{1,0:T(8,128)S(1)} %get-tuple-element.717) | copy-start | bytes 12292
  391.3 0.7 copy-start.18
  391.3 68.1 %copy-start = (bf16[256,4096]{1,0:T(8,128)(2,1)S(1)}, bf16[256,4096]{1,0:T(8,128)(2,1)}, u32[]{:S(2)}) copy-start(bf16[256,4096]{1,0:T(8,128)(2,1)} %param.16) | copy-start | bytes 6291460
  391.3 131.6 %all-gather.17.cloned.1.call-start = ((), (), s32[]{:S(2)}) async-start(), calls=%async_computation.8 | async-start | bytes 10485760 | tf_op jit(solution)/shard_map/all_gather | solution.py:103
  459.3 2.5 copy-start.5
  464.3 240.6 %reduce-scatter.7.cloned.1.call-start = ((), (), s32[]{:S(2)}) async-start(), calls=%async_computation.9 | async-start | bytes 10485760 | tf_op jit(solution)/shard_map/reduce_scatter | solution.py:106
  522.9 37.4 %copy-start.22 = (bf16[1024,4096]{1,0:T(8,128)(2,1)S(1)}, bf16[1024,4096]{1,0:T(8,128)(2,1)}, u32[]{:S(2)}) copy-start(bf16[1024,4096]{1,0:T(8,128)(2,1)} %all-gather.17.cloned.1.call-done) | copy-start | bytes 25165828
  634.1 70.8 %copy-start.1 = (bf16[256,4096]{1,0:T(8,128)(2,1)S(1)}, bf16[256,4096]{1,0:T(8,128)(2,1)}, u32[]{:S(2)}) copy-start(bf16[256,4096]{1,0:T(8,128)(2,1)} %param.16) | copy-start | bytes 6291460
  634.1 75.6 %copy-start.16 = (f32[1,4096]{1,0:T(1,128)S(1)}, f32[1,4096]{1,0:T(1,128)}, u32[]{:S(2)}) copy-start(f32[1,4096]{1,0:T(1,128)} %get-tuple-element.467) | copy-start | bytes 49156
  634.1 136.4 %all-gather.19.cloned.1.call-start = ((), (), s32[]{:S(2)}) async-start(), calls=%async_computation.10 | async-start | bytes 10485760 | tf_op jit(solution)/shard_map/all_gather | solution.py:89
  708.4 1.3 copy-start.2
  708.4 3.5 copy-start.12
  711.9 111.6 %all-gather.23.cloned.1.call-start = ((), (), s32[]{:S(2)}) async-start(), calls=%async_computation.12 | async-start | bytes 2621440 | tf_op jit(solution)/shard_map/all_gather | solution.py:98
  770.5 7.6 copy-start.11
  778.0 91.3 %all-gather.21.cloned.1.call-start = ((), (), s32[]{:S(2)}) async-start(), calls=%async_computation.11 | async-start | bytes 2621440 | tf_op jit(solution)/shard_map/all_gather | solution.py:97
  788.2 2.6 copy-start.8
  788.2 2.6 copy-start.10
  792.3 519.8 %reduce-scatter.9.cloned.1.call-start = ((), (), s32[]{:S(2)}) async-start(), calls=%async_computation.13 | async-start | bytes 10485760 | tf_op jit(solution)/shard_map/reduce_scatter | solution.py:101
  819.4 50.8 %copy-start.15 = (s32[4096]{0:T(1024)S(1)}, s32[4096]{0:T(1024)}, u32[]{:S(2)}) copy-start(s32[4096]{0:T(1024)} %copy-done.14) | copy-start | bytes 49156
  1242.2 69.8 %copy-start.3 = (bf16[256,4096]{1,0:T(8,128)(2,1)S(1)}, bf16[256,4096]{1,0:T(8,128)(2,1)}, u32[]{:S(2)}) copy-start(bf16[256,4096]{1,0:T(8,128)(2,1)} %copy-done.2) | copy-start | bytes 6291460
  1242.3 72.3 %copy-start.17 = (f32[1,4096]{1,0:T(1,128)S(1)}, f32[1,4096]{1,0:T(1,128)}, u32[]{:S(2)}) copy-start(f32[1,4096]{1,0:T(1,128)} %get-tuple-element.470) | copy-start | bytes 49156
  1242.3 133.4 %all-gather.25.cloned.1.call-start = ((), (), s32[]{:S(2)}) async-start(), calls=%async_computation.14 | async-start | bytes 10485760 | tf_op jit(solution)/shard_map/all_gather | solution.py:103
  1312.1 2.5 copy-start.6
  1317.0 240.5 %reduce-scatter.11.cloned.1.call-start = ((), (), s32[]{:S(2)}) async-start(), calls=%async_computation.15 | async-start | bytes 10485760 | tf_op jit(solution)/shard_map/reduce_scatter | solution.py:106
  1375.6 37.2 %copy-start.23 = (bf16[1024,4096]{1,0:T(8,128)(2,1)S(1)}, bf16[1024,4096]{1,0:T(8,128)(2,1)}, u32[]{:S(2)}) copy-start(bf16[1024,4096]{1,0:T(8,128)(2,1)} %all-gather.25.cloned.1.call-done) | copy-start | bytes 25165828
  1486.7 70.9 %copy-start.4 = (bf16[256,4096]{1,0:T(8,128)(2,1)S(1)}, bf16[256,4096]{1,0:T(8,128)(2,1)}, u32[]{:S(2)}) copy-start(bf16[256,4096]{1,0:T(8,128)(2,1)} %copy-done.2) | copy-start | bytes 6291460
Sparse Core Ops, SparseCore 0:
  13.7 61.2 all-gather.10
  85.5 45.2 all-gather.14
  132.4 44.2 all-gather.12
  391.4 67.8 reduce-scatter.4
  464.4 58.4 all-gather.16
  634.2 70.6 reduce-scatter.6
  712.0 58.4 all-gather.18
  778.1 45.2 all-gather.22
  825.0 44.2 all-gather.20
  1242.4 69.6 reduce-scatter.8
  1317.1 58.4 all-gather.24
  1486.8 70.6 reduce-scatter.10
where the time goes:
time: 1580 us; the launch traced here: 1570 us
  matrix products  726 us (46%)
  waiting for transfers between devices  535 us (34%)
  local copies, waits for them, and re-layouts  164 us (10%)
  other arithmetic  56.1 us (4%)
  loops' own time  45.8 us (3%)
  blocking collectives  26.6 us (2%)
    dot_general x14, matrix products, matmul(): return jnp.dot(rows_in, weight, preferred_element_type=jnp.float32)  304 us
    sub x64, matrix products, one_block(): attn_probs = jax.nn.softmax(scores, axis=-1).astype(jnp.bfloat16)  247 us
    dot_general x64, matrix products, one_block(): jnp.einsum('qgrk,kgd->qgrd', attn_probs, v_blk, preferred_element_type=jn...  174 us
    reduce_scatter x2, waiting for transfers between devices, local_fn(): mlp_out = lax.psum_scatter(part_sum, 'tp', scatter_dimension=0, tiled=True)  141 us
    reduce_scatter x2, waiting for transfers between devices, local_fn(): attn_out = lax.psum_scatter(part_sum, 'tp', scatter_dimension=0, tiled=True)  136 us
    all_gather x2, waiting for transfers between devices, local_fn(): normed = lax.all_gather(rms_norm(hidden, g_mlp[layer]), 'tp', tiled=True)  117 us
    all_gather x2, waiting for transfers between devices, local_fn(): normed = lax.all_gather(rms_norm(x, g_attn[layer]), 'tp', tiled=True)  92.6 us
    all_gather x2, waiting for transfers between devices, local_fn(): k_all = lax.all_gather(k, 'sp', tiled=True)  45.9 us
  transfers between devices with their start and end apart: 12, of which 10 were waited for; matrix products, arithmetic and copies ran while one was open for 9% of the time, Pallas kernels for 0%

commit v1 on v0

v1 whole, which is shorter than its diff:
```python
import functools

import jax
import jax.numpy as jnp
from jax import lax
from jax.experimental import pallas as pl
from jax.experimental.pallas import tpu as pltpu
from jax.sharding import PartitionSpec as P


EPS = 1e-6
ROPE_BASE = 10000.0
WINDOW = 1024
HEAD = 128
CHUNKS = 2
VMEM = 40 << 20
NEG = -1e30
LOG2E = 1.4426950408889634


def add_round(a, b):
    return (a.astype(jnp.float32) + b.astype(jnp.float32)).astype(jnp.bfloat16)


def relayout_kernel(sc_ref, wq_ref, wk_ref, wv_ref, q_ref, kv_ref, tmp_ref):
    q_ref[...] = pltpu.einshape("khd->k(hd)", wq_ref[0])
    width = kv_ref.shape[1] // 2
    start = pl.multiple_of(sc_ref[0] * width, width)
    for i, w in enumerate((wk_ref, wv_ref)):
        tmp_ref[i] = pltpu.einshape("khd->k(hd)", w[0])
        part = tmp_ref[i, :, pl.ds(start, width)]
        for h in range(width // HEAD):
            at = (2 * h + i) * HEAD
            kv_ref[:, at:at + HEAD] = part[:, h * HEAD:(h + 1) * HEAD]


def relayout(w_q, w_k, w_v, which, layer, kv_loc):
    _, k, heads, _ = w_q.shape
    kv_heads = w_k.shape[2]
    bk = 256
    return pl.pallas_call(
        relayout_kernel,
        grid_spec=pltpu.PrefetchScalarGridSpec(
            num_scalar_prefetch=1,
            grid=(k // bk,),
            in_specs=[pl.BlockSpec((1, bk, heads, HEAD), lambda i, s: (layer, i, 0, 0))]
            + [pl.BlockSpec((1, bk, kv_heads, HEAD), lambda i, s: (layer, i, 0, 0))] * 2,
            out_specs=[pl.BlockSpec((bk, heads * HEAD), lambda i, s: (i, 0)), pl.BlockSpec((bk, 2 * kv_loc * HEAD), lambda i, s: (i, 0))],
            scratch_shapes=[pltpu.VMEM((2, bk, kv_heads * HEAD), jnp.bfloat16)],
        ),
        out_shape=[jax.ShapeDtypeStruct((k, heads * HEAD), jnp.bfloat16), jax.ShapeDtypeStruct((k, 2 * kv_loc * HEAD), jnp.bfloat16)],
        cost_estimate=pl.CostEstimate(flops=10 ** 10, bytes_accessed=8 * k * heads * HEAD, transcendentals=0),
        compiler_params=pltpu.CompilerParams(vmem_limit_bytes=VMEM),
        name="relayout",
    )(which, w_q, w_k, w_v)


def norm_kernel(x_ref, s_ref, r_ref, g_ref, h_ref, n_ref):
    total = (s_ref[...].astype(jnp.float32) + r_ref[...].astype(jnp.float32)).astype(jnp.bfloat16)
    h = (x_ref[...].astype(jnp.float32) + total.astype(jnp.float32)).astype(jnp.bfloat16)
    h_ref[...] = h
    wide = h.astype(jnp.float32)
    inv_rms = lax.rsqrt(jnp.mean(wide * wide, axis=-1, keepdims=True) + EPS)
    n_ref[...] = (wide * inv_rms * g_ref[...]).astype(jnp.bfloat16)


def residual_norm(x, s, r, gain):
    rows, n = x.shape
    part = rows // 2
    here = pl.BlockSpec((part, n), lambda i: (i, 0))
    return pl.pallas_call(
        norm_kernel,
        grid=(2,),
        in_specs=[here, here, pl.BlockSpec((part, n), lambda i: (1 - i, 0)), pl.BlockSpec((1, n), lambda i: (0, 0))],
        out_specs=[here, here],
        out_shape=[jax.ShapeDtypeStruct((rows, n), jnp.bfloat16)] * 2,
        cost_estimate=pl.CostEstimate(flops=10 ** 8, bytes_accessed=10 * rows * n, transcendentals=0),
        compiler_params=pltpu.CompilerParams(vmem_limit_bytes=30 << 20),
        name="residual_norm",
    )(x, s, r, gain.astype(jnp.float32)[None])


def rotate(t, cos, sin):
    wide = t.astype(jnp.float32)
    return (wide * cos + pltpu.roll(wide, HEAD // 2, 1) * sin).astype(jnp.bfloat16)


def q_kernel(*refs):
    xs, (w_ref, cos_ref, sin_ref, o_ref) = refs[:2], refs[2:]
    x = jnp.concatenate([r[...] for r in xs], axis=0)
    t = jnp.dot(x, w_ref[...], preferred_element_type=jnp.float32).astype(jnp.bfloat16)
    for h in range(t.shape[1] // HEAD):
        cols = slice(h * HEAD, (h + 1) * HEAD)
        o_ref[:, cols] = rotate(t[:, cols], cos_ref[...], sin_ref[...])


def kv_kernel(*refs):
    xs, (w_ref, cos_ref, sin_ref), os = refs[:2], refs[2:5], refs[5:]
    step = pl.program_id(0)
    x = jnp.concatenate([r[...] for r in xs], axis=0)
    t = jnp.dot(x, w_ref[...], preferred_element_type=jnp.float32).astype(jnp.bfloat16)
    k = rotate(t[:, :HEAD], cos_ref[...], sin_ref[...])
    for h, o in enumerate(os):
        @pl.when(step == h)
        def _():
            o[:, :HEAD] = k
            o[:, HEAD:] = t[:, HEAD:]


def project(kernel, blocks, weight, cos_t, sin_t, outs):
    rows = sum(b.shape[0] for b in blocks)
    k, n = weight.shape
    bn = 2 * HEAD
    if outs == 1:
        out_specs = pl.BlockSpec((rows, bn), lambda j: (0, j))
        out_shape = jax.ShapeDtypeStruct((rows, n), jnp.bfloat16)
    else:
        out_specs = [pl.BlockSpec((rows, bn), lambda j: (0, 0))] * outs
        out_shape = [jax.ShapeDtypeStruct((rows, bn), jnp.bfloat16)] * outs
    return pl.pallas_call(
        kernel,
        grid=(n // bn,),
        in_specs=[pl.BlockSpec(b.shape, lambda j: (0, 0)) for b in blocks]
        + [pl.BlockSpec((k, bn), lambda j: (0, j))]
        + [pl.BlockSpec(cos_t.shape, lambda j: (0, 0))] * 2,
        out_specs=out_specs,
        out_shape=out_shape,
        cost_estimate=pl.CostEstimate(flops=2 * rows * k * n, bytes_accessed=2 * (k * n + rows * k), transcendentals=0),
        compiler_params=pltpu.CompilerParams(vmem_limit_bytes=VMEM),
    )(*blocks, weight, cos_t, sin_t)


def first_norm_kernel(a_ref, b_ref, g_ref, h_ref, n_ref):
    part = a_ref.shape[0]
    for i, r in enumerate((a_ref, b_ref)):
        rows = slice(i * part, (i + 1) * part)
        h_ref[rows] = r[...]
        wide = r[...].astype(jnp.float32)
        inv_rms = lax.rsqrt(jnp.mean(wide * wide, axis=-1, keepdims=True) + EPS)
        n_ref[rows] = (wide * inv_rms * g_ref[...]).astype(jnp.bfloat16)


def first_norm(a, b, gain):
    part, n = a.shape
    return pl.pallas_call(
        first_norm_kernel,
        out_shape=[jax.ShapeDtypeStruct((2 * part, n), jnp.bfloat16)] * 2,
        cost_estimate=pl.CostEstimate(flops=10 ** 8, bytes_accessed=12 * part * n, transcendentals=0),
        compiler_params=pltpu.CompilerParams(vmem_limit_bytes=30 << 20),
        name="first_norm",
    )(a, b, gain.astype(jnp.float32)[None])


def flash_kernel(chunk, windowed, n_rel, part, group, nh, scale, *refs):
    sc_ref, q_ref = refs[:2]
    count = CHUNKS * n_rel
    kv_in = refs[2:2 + nh * count]
    o_ref, kv_ref, m_ref, l_ref, acc_ref, sem = refs[2 + nh * count:]
    keys = 512 if windowed else 1024
    tile = pl.program_id(0)
    here, mine, cut1, cut2 = sc_ref[0], sc_ref[1], sc_ref[2], sc_ref[3]
    rows = part * CHUNKS

    @pl.when(tile == 0)
    def _():
        copies = []
        for g in range(nh):
            for c in range(CHUNKS):
                for rel in range(n_rel):
                    i = (g * CHUNKS + c) * n_rel + rel
                    for slot, flip in enumerate((0, 2, 1, 3)):
                        dst = pl.multiple_of(rel * 4 * rows + (mine ^ flip) * rows + c * part, part)
                        copies.append(pltpu.make_async_copy(kv_in[i].at[pl.ds(slot * part, part)], kv_ref.at[g, pl.ds(dst, part)], sem.at[4 * i + slot]))
        for c in copies:
            c.start()
        for c in copies:
            c.wait()

    m_ref[...] = jnp.full(m_ref.shape, NEG, jnp.float32)
    l_ref[...] = jnp.zeros(l_ref.shape, jnp.float32)
    acc_ref[...] = jnp.zeros(acc_ref.shape, jnp.float32)
    flip = 2 * (tile % 2) + tile // 2
    tok0 = here * 4 * rows + (mine ^ flip) * rows + chunk * part

    def lowest(tok):
        low = jnp.where(tok >= cut2, cut2, jnp.where(tok >= cut1, cut1, 0))
        return jnp.maximum(low, tok - (WINDOW - 1)) if windowed else low

    first, last = lowest(tok0) // keys, tok0 // keys
    tok = tok0 + lax.broadcasted_iota(jnp.int32, (part, HEAD), 0)
    lane = lax.broadcasted_iota(jnp.int32, (part, HEAD), 1)
    lower, upper = lowest(tok) - lane, tok - lane
    chains = m_ref.shape[0]
    heads = nh * group // chains

    def body(blk, carry):
        per = 4 * rows // keys
        start = pl.multiple_of((here - blk // per) * 4 * rows + (blk % per) * keys, keys)
        bias = []
        for i in range(keys // HEAD):
            base = blk * keys + i * HEAD
            bias.append(jnp.where((lower <= base) & (upper >= base), 0.0, NEG))
        bias = jnp.concatenate(bias, axis=1)
        scores, weights = [], []
        for j in range(chains):
            kb = kv_ref[j * nh // chains, pl.ds(start, keys), :HEAD]
            qs = jnp.concatenate([q_ref[:, h * HEAD:(h + 1) * HEAD] for h in range(j * heads, (j + 1) * heads)], axis=0)
            s = lax.dot_general(qs, kb, (((1,), (1,)), ((), ())), preferred_element_type=jnp.float32)
            scores.append((s.reshape(heads, part, keys) + bias[None]).reshape(heads * part, keys))
        for j in range(chains):
            m_old = m_ref[j]
            m_new = jnp.maximum(m_old, jnp.max(scores[j], axis=1, keepdims=True))
            alpha = jnp.exp2((m_old - m_new) * scale)
            p = jnp.exp2((scores[j] - jnp.concatenate([m_new] * (keys // HEAD), axis=1)) * scale)
            total = p[:, :HEAD]
            for i in range(1, keys // HEAD):
                total = total + p[:, i * HEAD:(i + 1) * HEAD]
            l_ref[j] = alpha * l_ref[j] + total
            m_ref[j] = m_new
            weights.append((alpha, p.astype(jnp.bfloat16)))
        for j in range(chains):
            alpha, p = weights[j]
            vb = kv_ref[j * nh // chains, pl.ds(start, keys), HEAD:]
            acc_ref[j] = alpha * acc_ref[j] + jnp.dot(p, vb, preferred_element_type=jnp.float32)
        return carry

    lax.fori_loop(first, last + 1, body, 0)
    for j in range(chains):
        out = (acc_ref[j] / jnp.sum(l_ref[j], axis=1, keepdims=True)).astype(jnp.bfloat16)
        for h in range(heads):
            o_ref[:, (j * heads + h) * HEAD:(j * heads + h + 1) * HEAD] = out[h * part:(h + 1) * part]


def flash(q, kv_pieces, scalars, chunk, windowed, head, kv_heads):
    rows = q.shape[0]
    nh = len(kv_pieces)
    width = q.shape[1] * nh // kv_heads
    flat = [p for pieces in kv_pieces for p in pieces]
    n_rel = len(kv_pieces[0]) // CHUNKS
    group = width // HEAD // nh
    part = rows // 4
    state = pltpu.VMEM((2, nh * group * part // 2, HEAD), jnp.float32)
    return pl.pallas_call(
        functools.partial(flash_kernel, chunk, windowed, n_rel, part, group, nh, HEAD ** -0.5 * LOG2E),
        grid_spec=pltpu.PrefetchScalarGridSpec(
            num_scalar_prefetch=1,
            grid=(4,),
            in_specs=[pl.BlockSpec((part, width), lambda i, s: (i, head))] + [pl.BlockSpec(memory_space=pl.ANY)] * len(flat),
            out_specs=pl.BlockSpec((part, width), lambda i, s: (i, 0)),
            scratch_shapes=[
                pltpu.VMEM((nh, CHUNKS * n_rel * rows, 2 * HEAD), jnp.bfloat16),
                state, state, state,
                pltpu.SemaphoreType.DMA((4 * len(flat),)),
            ],
        ),
        out_shape=jax.ShapeDtypeStruct((rows, width), jnp.bfloat16),
        cost_estimate=pl.CostEstimate(flops=10 ** 10, bytes_accessed=4 * rows * width, transcendentals=0),
        compiler_params=pltpu.CompilerParams(vmem_limit_bytes=VMEM),
        name="flash",
    )(scalars, q, *flat)


def out_kernel(n_in, *refs):
    w_ref, o_refs = refs[n_in], refs[n_in + 1:]
    x = jnp.concatenate([r[...] for r in refs[:n_in]], axis=1)
    t = jnp.dot(x, w_ref[0], preferred_element_type=jnp.float32).astype(jnp.bfloat16)
    rows = t.shape[0] // len(o_refs)
    for i, o in enumerate(o_refs):
        o[...] = t[i * rows:(i + 1) * rows]


def project_out(mixed, weight, layer):
    rows = mixed[0].shape[0]
    k, n = weight.shape[1:]
    bn = 1024
    part = rows // 2
    return pl.pallas_call(
        functools.partial(out_kernel, len(mixed)),
        grid=(n // bn,),
        in_specs=[pl.BlockSpec(m.shape, lambda j: (0, 0)) for m in mixed] + [pl.BlockSpec((1, k, bn), lambda j: (layer, 0, j))],
        out_specs=[pl.BlockSpec((part, bn), lambda j: (0, j))] * 2,
        out_shape=[jax.ShapeDtypeStruct((part, n), jnp.bfloat16)] * 2,
        cost_estimate=pl.CostEstimate(flops=2 * rows * k * n, bytes_accessed=2 * (k * n + rows * k), transcendentals=0),
        compiler_params=pltpu.CompilerParams(vmem_limit_bytes=VMEM),
        name="out_proj",
    )(*mixed, weight)


def mlp_kernel(*refs):
    xs, (wg_ref, wu_ref, wd_ref), os, acc_ref = refs[:2], refs[2:5], refs[5:7], refs[7]
    step = pl.program_id(0)
    x = jnp.concatenate([r[...] for r in xs], axis=0)
    gate = jnp.dot(x, wg_ref[0], preferred_element_type=jnp.float32)
    up = jnp.dot(x, wu_ref[0], preferred_element_type=jnp.float32)
    act = (jax.nn.silu(gate) * up).astype(jnp.bfloat16)
    n = wd_ref.shape[2]
    bn = 1024
    part = x.shape[0] // 2
    last = pl.num_programs(0) - 1

    def each(fn):
        for c in range(0, n, bn):
            fn(slice(c, c + bn), jnp.dot(act, wd_ref[0, :, c:c + bn], preferred_element_type=jnp.float32))

    @pl.when(step == 0)
    def _():
        def put(cols, t):
            acc_ref[:, cols] = t

        each(put)

    @pl.when((step > 0) & (step < last))
    def _():
        def put(cols, t):
            acc_ref[:, cols] += t

        each(put)

    @pl.when(step == last)
    def _():
        def put(cols, t):
            t = (acc_ref[:, cols] + t).astype(jnp.bfloat16)
            for i, o in enumerate(os):
                o[:, cols] = t[i * part:(i + 1) * part]

        each(put)


def mlp(blocks, wg, wu, wd, layer):
    part, k = blocks[0].shape
    rows = 2 * part
    ff = wg.shape[2]
    n = wd.shape[2]
    bf = 256
    return pl.pallas_call(
        mlp_kernel,
        grid=(ff // bf,),
        in_specs=[pl.BlockSpec((part, k), lambda j: (0, 0))] * 2
        + [pl.BlockSpec((1, k, bf), lambda j: (layer, 0, j))] * 2
        + [pl.BlockSpec((1, bf, n), lambda j: (layer, j, 0))],
        out_specs=[pl.BlockSpec((part, n), lambda j: (0, 0))] * 2,
        out_shape=[jax.ShapeDtypeStruct((part, n), jnp.bfloat16)] * 2,
        scratch_shapes=[pltpu.VMEM((rows, n), jnp.float32)],
        cost_estimate=pl.CostEstimate(flops=6 * rows * k * ff, bytes_accessed=6 * k * ff, transcendentals=rows * ff),
        compiler_params=pltpu.CompilerParams(vmem_limit_bytes=58 << 20),
        name="mlp",
    )(*blocks, wg, wu, wd)


def solution(mesh):
    tp_size, sp_size = mesh.shape["tp"], mesh.shape["sp"]
    row_spec = P(("dp", "sp", "tp"), None)
    id_spec = P(("dp", "sp", "tp"))
    whole = P()
    in_specs = (row_spec, id_spec, id_spec, whole, P(None, None, "tp", None), whole, whole, P(None, "tp", None, None), whole, P(None, None, "tp"), P(None, None, "tp"), P(None, "tp", None))
    near = [(i, i ^ 1) for i in range(tp_size)]
    across = [(i, i ^ 2) for i in range(tp_size)]

    def local_fn(x, segment_ids, positions, g_attn, w_q, w_k, w_v, w_o, g_mlp, w_gate, w_up, w_down):
        sp_idx = lax.axis_index("sp")
        tp_idx = lax.axis_index("tp")
        layers, model, heads_loc, _ = w_q.shape
        kv_heads = w_k.shape[2] // tp_size
        rows = x.shape[0]
        part = rows // CHUNKS
        group_rows = rows * tp_size
        order = [tp_idx, tp_idx ^ 2, tp_idx ^ 1, tp_idx ^ 3]
        which = tp_idx.astype(jnp.int32)[None]

        ids = lax.all_gather(jnp.stack([segment_ids, positions]), ("sp", "tp"))
        x, ids = lax.optimization_barrier((x, ids))
        own = [x[c * part:(c + 1) * part] for c in range(CHUNKS)]
        resid, normed = [], []
        for c in range(CHUNKS):
            other = lax.ppermute(own[c], "tp", across)
            pair = first_norm(own[c], other, g_attn[0])
            resid.append(pair[0])
            normed.append(pair[1])

        seg_all = ids[:, 0].reshape(-1)
        starts = [jnp.sum((seg_all < s).astype(jnp.int32)) for s in (1, 2)]
        pos_here = lax.dynamic_slice_in_dim(ids[:, 1], sp_idx * tp_size, tp_size, 0)
        half = HEAD // 2
        inv_freq = ROPE_BASE ** (-jnp.arange(half, dtype=jnp.float32) / half)
        inv_freq = jnp.concatenate([inv_freq, inv_freq])
        sign = jnp.where(jnp.arange(HEAD) < half, -1.0, 1.0)
        cos_t, sin_t = [], []
        pos_rel = jnp.concatenate([lax.dynamic_slice_in_dim(pos_here, o, 1, 0) for o in order])
        for c in range(CHUNKS):
            pos = pos_rel[:, c * part:(c + 1) * part].reshape(-1)
            angles = pos.astype(jnp.float32)[:, None] * inv_freq[None, :]
            cos_t.append(jnp.cos(angles))
            sin_t.append(jnp.sin(angles) * sign[None, :])
        scalars = jnp.stack([sp_idx.astype(jnp.int32), tp_idx.astype(jnp.int32)] + starts)

        wo_flat = w_o.reshape(layers, heads_loc * HEAD, model)
        wq_l, wkv_l = [], []
        for layer in range(layers):
            a, b = relayout(w_q, w_k, w_v, which, layer, kv_heads)
            wq_l.append(a)
            wkv_l.append(b)

        def share(n):
            return [n, lax.ppermute(n, "tp", near)]

        def exchange(parts):
            theirs = lax.ppermute(parts[1], "tp", near)
            s = add_round(parts[0], theirs)
            return s, lax.ppermute(s, "tp", across)

        def exchange_last(parts, x_blk):
            theirs = lax.ppermute(parts[1], "tp", near)
            s = add_round(parts[0], theirs)
            r = lax.ppermute(s[part:], "tp", across)
            return add_round(x_blk[:part], add_round(s[:part], r))

        out = []
        for layer in range(layers):
            windowed = layer % 2 == 0
            shifts = min(WINDOW // group_rows, sp_size - 1) if windowed else sp_size - 1
            q, kv = [], [[] for _ in range(kv_heads)]
            for c in range(CHUNKS):
                full = share(normed[c])
                mine = project(kv_kernel, full, wkv_l[layer], cos_t[c], sin_t[c], kv_heads)
                for h in range(kv_heads):
                    kv[h].append(mine[h])
                    for s in range(1, shifts + 1):
                        kv[h].append(lax.ppermute(mine[h], "sp", [(z, z + s) for z in range(sp_size - s)]))
                q.append(project(q_kernel, full, wq_l[layer], cos_t[c], sin_t[c], 1))
            for c in range(CHUNKS):
                mixed = []
                for h in range(1 if windowed else kv_heads):
                    mixed.append(flash(q[c], kv if windowed else [kv[h]], scalars, c, windowed, h, kv_heads))
                parts = project_out(mixed, wo_flat, layer)
                s, r = exchange(parts)
                resid[c], normed[c] = residual_norm(resid[c], s, r, g_mlp[layer])
            for c in range(CHUNKS):
                full = share(normed[c])
                parts = mlp(full, w_gate, w_up, w_down, layer)
                if layer == layers - 1:
                    out.append(exchange_last(parts, resid[c]))
                else:
                    s, r = exchange(parts)
                    resid[c], normed[c] = residual_norm(resid[c], s, r, g_attn[layer + 1])
        return jnp.concatenate(out, axis=0)

    return jax.shard_map(local_fn, mesh=mesh, in_specs=in_specs, out_specs=row_spec, check_vma=False)
```

time: 1580 us -> 939 us (0.59)
  the two profiles are of different devices: /device:TPU:0 before, /device:TPU:10 now
where the time goes in v1:
time: 939 us; the launch traced here: 931 us
  Pallas kernels  440 us (47%)
  waiting for transfers between devices  388 us (41%)
  starting transfers between devices  39.7 us (4%)
  local copies, waits for them, and re-layouts  24.5 us (3%)
  blocking collectives  18.9 us (2%)
  other arithmetic  18.5 us (2%)
    ppermute x6, waiting for transfers between devices, exchange(): return (s, lax.ppermute(s, 'tp', across))  261 us
    pallas_call x4, Pallas kernels, mlp(): pl.pallas_call(mlp_kernel, grid=(ff // bf,), in_specs=[pl.BlockSpec((part...  232 us
    pallas_call x6, Pallas kernels, flash(): pl.pallas_call(functools.partial(flash_kernel, chunk, windowed, n_rel, pa...  82.6 us
    pallas_call x8, Pallas kernels, project(): pl.pallas_call(kernel, grid=(n // bn,), in_specs=[pl.BlockSpec(b.shape, l...  50.5 us
    ppermute x2, waiting for transfers between devices, exchange_last(): r = lax.ppermute(s[part:], 'tp', across)  44.1 us
    ppermute x2, waiting for transfers between devices, local_fn(): other = lax.ppermute(own[c], 'tp', across)  42.4 us
    ppermute x16, waiting for transfers between devices, local_fn(): lax.ppermute(mine[h], 'sp', [(z, z + s) for z in range(sp_size - s)])  33.8 us
    ppermute x16, starting transfers between devices, local_fn(): lax.ppermute(mine[h], 'sp', [(z, z + s) for z in range(sp_size - s)])  31.1 us
  transfers between devices with their start and end apart: 42, of which 20 were waited for; matrix products, arithmetic and copies ran while one was open for 2% of the time, Pallas kernels for 43%

profile of v1, /device:TPU:10, one launch (start us, length us, event | category | flops | bytes accessed | tf_op | source)
XLA Modules:
  0.0 930.8 jit_solution(4512851725857626886)
XLA Ops:
  0.7 18.9 %all-gather.1 = s32[16,2,256]{2,1,0:T(2,128)S(1)} all-gather(s32[1,2,256]{2,1,0:T(2,128)S(1)} %add_bitcast_fusion), channel_id=2, replica_groups=mesh['dp'=2,'sp'=4,'tp'=4] {'sp','tp'}, dimensions={0}, use_global_device_ids=true | all-gather | bytes 34816 | tf_op jit(solution)/shard_map/all_gather | solution.py:370
  23.4 24.0 %collective-permute-done.b_ref = bf16[128,4096]{1,0:T(8,128)(2,1)S(1)} collective-permute-done((bf16[128,4096]{1,0:T(8,128)(2,1)S(1)}, bf16[128,4096]{1,0:T(8,128)(2,1)S(1)}, u32[]{:S(2)}, u32[]{:S(2)}) %collective-permute-start) | collective-permute-done | bytes 1048608 | tf_op jit(solution)/shard_map/ppermute | solution.py:375
  47.4 2.6 first_norm.2
  50.8 18.5 %collective-permute-done.3.b_ref = bf16[128,4096]{1,0:T(8,128)(2,1)S(1)} collective-permute-done((bf16[128,4096]{1,0:T(8,128)(2,1)S(1)}, bf16[128,4096]{1,0:T(8,128)(2,1)S(1)}, u32[]{:S(2)}, u32[]{:S(2)}) %collective-permute-start.3) | collective-permute-done | bytes 1048608 | tf_op jit(solution)/shard_map/ppermute | solution.py:375
  76.6 14.7 %relayout.2 = (bf16[4096,1024]{1,0:T(8,128)(2,1)S(1)}, bf16[4096,512]{1,0:T(8,128)(2,1)S(1)}) custom-call(s32[1]{0:T(128)} %bitcast.4.sc_ref, bf16[2,4096,8,128]{3,2,1,0:T(8,128)(2,1)} %wq_ref.3, bf16[2,4096,8,128]{3,2,1,0:T(8,128)(2,1)} %wk_ref.3, bf16[2,4096,8,128]{3,2,1,0:T(8,128)(2,1)} %wv_ref.3), custom_call_target="tpu_custom_call" | custom-call | flops 10000000000 | bytes 33554432 | tf_op jit(solution)/shard_map/relayout/pallas_call | solution.py:41
  91.3 3.3 copy-done.18
  94.6 5.1 shard_map.119
  101.7 5.1 shard_map.120
  106.9 3.0 collective-permute-start.5
  114.0 3.4 copy-done.19
  117.4 8.5 shard_map.118.refs_1_
  125.9 3.1 collective-permute-done.7.refs_9_
  129.0 16.7 %flash.6.refs_0_ = bf16[512,1024]{1,0:T(8,128)(2,1)S(1)} custom-call(s32[4]{0:T(128)S(1)} %pad_add_fusion.1.refs_0_, bf16[512,1024]{1,0:T(8,128)(2,1)S(1)} %shard_map.118.refs_1_, bf16[512,256]{1,0:T(8,128)(2,1)S(1)} %get-tuple-element.57.refs_2_, bf16[512,256]{1,0:T(8,128)(2,1)S(1)} %collective-permute-done.2.refs_3_, ...), custom_call_target="tpu_custom_call" | custom-call | flops 10000000000 | bytes 2097152 | tf_op jit(solution)/shard_map/flash/pallas_call | solution.py:243
  145.7 7.2 out_proj.4
  153.0 3.4 copy-done.20
  156.3 8.5 shard_map.123.refs_1_
  164.9 16.7 %flash.7.refs_0_ = bf16[512,1024]{1,0:T(8,128)(2,1)S(1)} custom-call(s32[4]{0:T(128)S(1)} %pad_add_fusion.1.refs_0_, bf16[512,1024]{1,0:T(8,128)(2,1)S(1)} %shard_map.123.refs_1_, bf16[512,256]{1,0:T(8,128)(2,1)S(1)} %get-tuple-element.57.refs_2_, bf16[512,256]{1,0:T(8,128)(2,1)S(1)} %collective-permute-done.2.refs_3_, ...), custom_call_target="tpu_custom_call" | custom-call | flops 10000000000 | bytes 2097152 | tf_op jit(solution)/shard_map/flash/pallas_call | solution.py:243
  181.6 7.2 out_proj.5
  194.7 45.6 %collective-permute-done.9.r_ref = bf16[256,4096]{1,0:T(8,128)(2,1)S(1)} collective-permute-done((bf16[256,4096]{1,0:T(8,128)(2,1)S(1)}, bf16[256,4096]{1,0:T(8,128)(2,1)S(1)}, u32[]{:S(2)}, u32[]{:S(2)}) %collective-permute-start.9) | collective-permute-done | bytes 2097184 | tf_op jit(solution)/shard_map/ppermute | solution.py:409
  243.3 41.0 %collective-permute-done.18.r_ref = bf16[256,4096]{1,0:T(8,128)(2,1)S(1)} collective-permute-done((bf16[256,4096]{1,0:T(8,128)(2,1)S(1)}, bf16[256,4096]{1,0:T(8,128)(2,1)S(1)}, u32[]{:S(2)}, u32[]{:S(2)}) %collective-permute-start.18) | collective-permute-done | bytes 2097184 | tf_op jit(solution)/shard_map/ppermute | solution.py:409
  287.3 58.3 %mlp.4 = (bf16[256,4096]{1,0:T(8,128)(2,1)}, bf16[256,4096]{1,0:T(8,128)(2,1)}) custom-call(bf16[256,4096]{1,0:T(8,128)(2,1)} %copy-done.4, bf16[256,4096]{1,0:T(8,128)(2,1)} %collective-permute-done.10.refs_1_, bf16[2,4096,3584]{2,1,0:T(8,128)(2,1)} %refs_2_.7, bf16[2,4096,3584]{2,1,0:T(8,128)(2,1)} %refs_3_.7, bf16[2,3584,4096]{2,1,0:T(8,128)(2,1)} %refs_4_.7), custom_call_target="tpu_custom_call" | custom-call | flops 45097156608 | bytes 88080384 | tf_op jit(solution)/shard_map/mlp/pallas_call | solution.py:335
  346.0 57.8 %mlp.5 = (bf16[256,4096]{1,0:T(8,128)(2,1)}, bf16[256,4096]{1,0:T(8,128)(2,1)}) custom-call(bf16[256,4096]{1,0:T(8,128)(2,1)} %copy-done.6, bf16[256,4096]{1,0:T(8,128)(2,1)} %collective-permute-done.19.refs_1_, bf16[2,4096,3584]{2,1,0:T(8,128)(2,1)} %refs_2_.7, bf16[2,4096,3584]{2,1,0:T(8,128)(2,1)} %refs_3_.7, bf16[2,3584,4096]{2,1,0:T(8,128)(2,1)} %refs_4_.7), custom_call_target="tpu_custom_call" | custom-call | flops 45097156608 | bytes 88080384 | tf_op jit(solution)/shard_map/mlp/pallas_call | solution.py:335
  409.6 45.6 %collective-permute-done.12.r_ref = bf16[256,4096]{1,0:T(8,128)(2,1)S(1)} collective-permute-done((bf16[256,4096]{1,0:T(8,128)(2,1)S(1)}, bf16[256,4096]{1,0:T(8,128)(2,1)S(1)}, u32[]{:S(2)}, u32[]{:S(2)}) %collective-permute-start.12) | collective-permute-done | bytes 2097184 | tf_op jit(solution)/shard_map/ppermute | solution.py:409
  457.0 42.4 %collective-permute-done.21.r_ref = bf16[256,4096]{1,0:T(8,128)(2,1)S(1)} collective-permute-done((bf16[256,4096]{1,0:T(8,128)(2,1)S(1)}, bf16[256,4096]{1,0:T(8,128)(2,1)S(1)}, u32[]{:S(2)}, u32[]{:S(2)}) %collective-permute-start.21) | collective-permute-done | bytes 2097184 | tf_op jit(solution)/shard_map/ppermute | solution.py:409
  499.4 2.8 residual_norm.9
  502.3 14.6 %relayout.3 = (bf16[4096,1024]{1,0:T(8,128)(2,1)S(1)}, bf16[4096,512]{1,0:T(8,128)(2,1)S(1)}) custom-call(s32[1]{0:T(128)} %bitcast.4.sc_ref, bf16[2,4096,8,128]{3,2,1,0:T(8,128)(2,1)} %wq_ref.3, bf16[2,4096,8,128]{3,2,1,0:T(8,128)(2,1)} %wk_ref.3, bf16[2,4096,8,128]{3,2,1,0:T(8,128)(2,1)} %wv_ref.3), custom_call_target="tpu_custom_call" | custom-call | flops 10000000000 | bytes 33554432 | tf_op jit(solution)/shard_map/relayout/pallas_call | solution.py:41
  516.9 3.1 shard_map.122
  524.1 5.1 shard_map.124
  533.2 3.4 copy-done.22
  536.6 8.5 shard_map.125.refs_1_
  548.9 6.6 shard_map.121.refs_1_
  557.1 3.5 collective-permute-start.27
  563.2 16.2 %collective-permute-done.24.refs_8_ = bf16[512,256]{1,0:T(8,128)(2,1)} collective-permute-done((bf16[512,256]{1,0:T(8,128)(2,1)S(1)}, bf16[512,256]{1,0:T(8,128)(2,1)}, u32[]{:S(2)}, u32[]{:S(2)}) %collective-permute-start.24) | collective-permute-done | bytes 262176 | tf_op jit(solution)/shard_map/ppermute | solution.py:428
  581.3 4.8 collective-permute-start.30
  587.7 12.4 %flash.10.refs_0_ = bf16[512,512]{1,0:T(8,128)(2,1)S(1)} custom-call(s32[4]{0:T(128)S(1)} %pad_add_fusion.1.refs_0_, bf16[512,1024]{1,0:T(8,128)(2,1)S(1)} %copy-done.30, bf16[512,256]{1,0:T(8,128)(2,1)S(1)} %get-tuple-element.72.refs_2_, bf16[512,256]{1,0:T(8,128)(2,1)S(1)} %collective-permute-done.14.refs_3_, ...), custom_call_target="tpu_custom_call" | custom-call | flops 10000000000 | bytes 1048576 | tf_op jit(solution)/shard_map/flash/pallas_call | solution.py:243
  601.9 5.6 collective-permute-done.29.refs_7_
  607.5 5.4 collective-permute-done.30.refs_8_
  612.9 12.2 %flash.11.refs_1_ = bf16[512,512]{1,0:T(8,128)(2,1)S(1)} custom-call(s32[4]{0:T(128)S(1)} %pad_add_fusion.1.refs_0_, bf16[512,1024]{1,0:T(8,128)(2,1)S(1)} %copy-done.30, bf16[512,256]{1,0:T(8,128)(2,1)S(1)} %get-tuple-element.82.refs_2_, bf16[512,256]{1,0:T(8,128)(2,1)S(1)} %collective-permute-done.26.refs_3_, ...), custom_call_target="tpu_custom_call" | custom-call | flops 10000000000 | bytes 1048576 | tf_op jit(solution)/shard_map/flash/pallas_call | solution.py:243
  625.1 7.3 out_proj.7
  632.5 12.2 %flash.8.refs_0_ = bf16[512,512]{1,0:T(8,128)(2,1)S(1)} custom-call(s32[4]{0:T(128)S(1)} %pad_add_fusion.1.refs_0_, bf16[512,1024]{1,0:T(8,128)(2,1)S(1)} %copy-done.28, bf16[512,256]{1,0:T(8,128)(2,1)S(1)} %get-tuple-element.72.refs_2_, bf16[512,256]{1,0:T(8,128)(2,1)S(1)} %collective-permute-done.14.refs_3_, ...), custom_call_target="tpu_custom_call" | custom-call | flops 10000000000 | bytes 1048576 | tf_op jit(solution)/shard_map/flash/pallas_call | solution.py:243
  644.8 12.2 %flash.9.refs_1_ = bf16[512,512]{1,0:T(8,128)(2,1)S(1)} custom-call(s32[4]{0:T(128)S(1)} %pad_add_fusion.1.refs_0_, bf16[512,1024]{1,0:T(8,128)(2,1)S(1)} %copy-done.28, bf16[512,256]{1,0:T(8,128)(2,1)S(1)} %get-tuple-element.82.refs_2_, bf16[512,256]{1,0:T(8,128)(2,1)S(1)} %collective-permute-done.26.refs_3_, ...), custom_call_target="tpu_custom_call" | custom-call | flops 10000000000 | bytes 1048576 | tf_op jit(solution)/shard_map/flash/pallas_call | solution.py:243
  657.0 7.2 out_proj.6
  669.7 44.4 %collective-permute-done.38.r_ref = bf16[256,4096]{1,0:T(8,128)(2,1)S(1)} collective-permute-done((bf16[256,4096]{1,0:T(8,128)(2,1)S(1)}, bf16[256,4096]{1,0:T(8,128)(2,1)S(1)}, u32[]{:S(2)}, u32[]{:S(2)}) %collective-permute-start.38) | collective-permute-done | bytes 2097184 | tf_op jit(solution)/shard_map/ppermute | solution.py:409
  716.0 42.2 %collective-permute-done.33.r_ref = bf16[256,4096]{1,0:T(8,128)(2,1)S(1)} collective-permute-done((bf16[256,4096]{1,0:T(8,128)(2,1)S(1)}, bf16[256,4096]{1,0:T(8,128)(2,1)S(1)}, u32[]{:S(2)}, u32[]{:S(2)}) %collective-permute-start.33) | collective-permute-done | bytes 2097184 | tf_op jit(solution)/shard_map/ppermute | solution.py:409
  761.2 58.3 %mlp.7 = (bf16[256,4096]{1,0:T(8,128)(2,1)}, bf16[256,4096]{1,0:T(8,128)(2,1)}) custom-call(bf16[256,4096]{1,0:T(8,128)(2,1)} %copy-done.5, bf16[256,4096]{1,0:T(8,128)(2,1)} %collective-permute-done.39.refs_1_, bf16[2,4096,3584]{2,1,0:T(8,128)(2,1)} %refs_2_.7, bf16[2,4096,3584]{2,1,0:T(8,128)(2,1)} %refs_3_.7, bf16[2,3584,4096]{2,1,0:T(8,128)(2,1)} %refs_4_.7), custom_call_target="tpu_custom_call" | custom-call | flops 45097156608 | bytes 88080384 | tf_op jit(solution)/shard_map/mlp/pallas_call | solution.py:335
  819.6 58.0 %mlp.6 = (bf16[256,4096]{1,0:T(8,128)(2,1)}, bf16[256,4096]{1,0:T(8,128)(2,1)}) custom-call(bf16[256,4096]{1,0:T(8,128)(2,1)} %copy-done.7, bf16[256,4096]{1,0:T(8,128)(2,1)} %collective-permute-done.34.refs_1_, bf16[2,4096,3584]{2,1,0:T(8,128)(2,1)} %refs_2_.7, bf16[2,4096,3584]{2,1,0:T(8,128)(2,1)} %refs_3_.7, bf16[2,3584,4096]{2,1,0:T(8,128)(2,1)} %refs_4_.7), custom_call_target="tpu_custom_call" | custom-call | flops 45097156608 | bytes 88080384 | tf_op jit(solution)/shard_map/mlp/pallas_call | solution.py:335
  883.7 23.0 %collective-permute-done.41 = bf16[128,4096]{1,0:T(8,128)(2,1)S(1)} collective-permute-done((bf16[128,4096]{1,0:T(8,128)(2,1)S(1)}, bf16[128,4096]{1,0:T(8,128)(2,1)S(1)}, u32[]{:S(2)}, u32[]{:S(2)}) %collective-permute-start.41) | collective-permute-done | bytes 1048608 | tf_op jit(solution)/shard_map/ppermute | solution.py:414
  907.2 21.1 %collective-permute-done.36 = bf16[128,4096]{1,0:T(8,128)(2,1)S(1)} collective-permute-done((bf16[128,4096]{1,0:T(8,128)(2,1)S(1)}, bf16[128,4096]{1,0:T(8,128)(2,1)S(1)}, u32[]{:S(2)}, u32[]{:S(2)}) %collective-permute-start.36) | collective-permute-done | bytes 1048608 | tf_op jit(solution)/shard_map/ppermute | solution.py:414
  (168 shorter events, 78.5 us)
Async XLA Ops:
  21.3 26.1 %collective-permute-start = (bf16[128,4096]{1,0:T(8,128)(2,1)S(1)}, bf16[128,4096]{1,0:T(8,128)(2,1)S(1)}, u32[]{:S(2)}, u32[]{:S(2)}) collective-permute-start(bf16[128,4096]{1,0:T(8,128)(2,1)S(1)} %get-tuple-element.99.a_ref), channel_id=1, source_target_pairs={{0,2},{1,3},{2,0},{3,1},{4,6},{5,7},{6,4},{7,5},{8,10},{9,11},{10,... | collective-permute-start | bytes 3145736 | tf_op jit(solution)/shard_map/ppermute | solution.py:375
  21.4 47.9 %collective-permute-start.3 = (bf16[128,4096]{1,0:T(8,128)(2,1)S(1)}, bf16[128,4096]{1,0:T(8,128)(2,1)S(1)}, u32[]{:S(2)}, u32[]{:S(2)}) collective-permute-start(bf16[128,4096]{1,0:T(8,128)(2,1)S(1)} %get-tuple-element.100.a_ref), channel_id=1, source_target_pairs={{0,2},{1,3},{2,0},{3,1},{4,6},{5,7},{6,4},{7,5},{8,10},{9,11},{10,... | collective-permute-start | bytes 3145736 | tf_op jit(solution)/shard_map/ppermute | solution.py:375
  50.0 44.6 %collective-permute-start.1 = (bf16[256,4096]{1,0:T(8,128)(2,1)}, bf16[256,4096]{1,0:T(8,128)(2,1)}, u32[]{:S(2)}, u32[]{:S(2)}) collective-permute-start(bf16[256,4096]{1,0:T(8,128)(2,1)} %get-tuple-element.54.refs_0_), channel_id=1, source_target_pairs={{0,1},{1,0},{2,3},{3,2},{4,5},{5,4},{6,7},{7,6},{8,9},{9,8},{10,11... | collective-permute-start | bytes 6291464 | tf_op jit(solution)/shard_map/ppermute | solution.py:404
  73.1 28.6 %collective-permute-start.4 = (bf16[256,4096]{1,0:T(8,128)(2,1)}, bf16[256,4096]{1,0:T(8,128)(2,1)}, u32[]{:S(2)}, u32[]{:S(2)}) collective-permute-start(bf16[256,4096]{1,0:T(8,128)(2,1)} %get-tuple-element.58.refs_0_), channel_id=1, source_target_pairs={{0,1},{1,0},{2,3},{3,2},{4,5},{5,4},{6,7},{7,6},{8,9},{9,8},{10,11... | collective-permute-start | bytes 6291464 | tf_op jit(solution)/shard_map/ppermute | solution.py:404
  99.8 26.1 %collective-permute-start.2 = (bf16[512,256]{1,0:T(8,128)(2,1)S(1)}, bf16[512,256]{1,0:T(8,128)(2,1)S(1)}, u32[]{:S(2)}, u32[]{:S(2)}) collective-permute-start(bf16[512,256]{1,0:T(8,128)(2,1)S(1)} %get-tuple-element.57.refs_2_), channel_id=1, source_target_pairs={{0,4},{4,8},{8,12},{1,5},{5,9},{9,13},{2,6},{6,10},{10,14},{3,7},{... | collective-permute-start | bytes 786440 | tf_op jit(solution)/shard_map/ppermute | solution.py:428
  106.9 19.0 %collective-permute-start.5 = (bf16[512,256]{1,0:T(8,128)(2,1)S(1)}, bf16[512,256]{1,0:T(8,128)(2,1)S(1)}, u32[]{:S(2)}, u32[]{:S(2)}) collective-permute-start(bf16[512,256]{1,0:T(8,128)(2,1)S(1)} %get-tuple-element.59.refs_4_), channel_id=1, source_target_pairs={{0,4},{4,8},{8,12},{1,5},{5,9},{9,13},{2,6},{6,10},{10,14},{3,7},{... | collective-permute-start | bytes 786440 | tf_op jit(solution)/shard_map/ppermute | solution.py:428
  109.9 16.0 %collective-permute-start.6 = (bf16[512,256]{1,0:T(8,128)(2,1)S(1)}, bf16[512,256]{1,0:T(8,128)(2,1)S(1)}, u32[]{:S(2)}, u32[]{:S(2)}) collective-permute-start(bf16[512,256]{1,0:T(8,128)(2,1)S(1)} %get-tuple-element.60.refs_6_), channel_id=1, source_target_pairs={{0,4},{4,8},{8,12},{1,5},{5,9},{9,13},{2,6},{6,10},{10,14},{3,7},{... | collective-permute-start | bytes 786440 | tf_op jit(solution)/shard_map/ppermute | solution.py:428
  111.8 17.1 %collective-permute-start.7 = (bf16[512,256]{1,0:T(8,128)(2,1)S(1)}, bf16[512,256]{1,0:T(8,128)(2,1)S(1)}, u32[]{:S(2)}, u32[]{:S(2)}) collective-permute-start(bf16[512,256]{1,0:T(8,128)(2,1)S(1)} %get-tuple-element.61.refs_8_), channel_id=1, source_target_pairs={{0,4},{4,8},{8,12},{1,5},{5,9},{9,13},{2,6},{6,10},{10,14},{3,7},{... | collective-permute-start | bytes 786440 | tf_op jit(solution)/shard_map/ppermute | solution.py:428
  152.9 36.5 %collective-permute-start.8 = (bf16[256,4096]{1,0:T(8,128)(2,1)S(1)}, bf16[256,4096]{1,0:T(8,128)(2,1)}, u32[]{:S(2)}, u32[]{:S(2)}) collective-permute-start(bf16[256,4096]{1,0:T(8,128)(2,1)S(1)} %get-tuple-element.63), channel_id=1, source_target_pairs={{0,1},{1,0},{2,3},{3,2},{4,5},{5,4},{6,7},{7,6},{8,9},{9,8},{10,11... | collective-permute-start | bytes 6291464 | tf_op jit(solution)/shard_map/ppermute | solution.py:407
  188.8 4.3 collective-permute-start.17
  191.7 48.6 %collective-permute-start.9 = (bf16[256,4096]{1,0:T(8,128)(2,1)S(1)}, bf16[256,4096]{1,0:T(8,128)(2,1)S(1)}, u32[]{:S(2)}, u32[]{:S(2)}) collective-permute-start(bf16[256,4096]{1,0:T(8,128)(2,1)S(1)} %add_convert_fusion.7.s_ref), channel_id=1, source_target_pairs={{0,2},{1,3},{2,0},{3,1},{4,6},{5,7},{6,4},{7,5},{8,10},{9,11},{10,... | collective-permute-start | bytes 6291464 | tf_op jit(solution)/shard_map/ppermute | solution.py:409
  193.9 90.4 %collective-permute-start.18 = (bf16[256,4096]{1,0:T(8,128)(2,1)S(1)}, bf16[256,4096]{1,0:T(8,128)(2,1)S(1)}, u32[]{:S(2)}, u32[]{:S(2)}) collective-permute-start(bf16[256,4096]{1,0:T(8,128)(2,1)S(1)} %add_convert_fusion.5.s_ref), channel_id=1, source_target_pairs={{0,2},{1,3},{2,0},{3,1},{4,6},{5,7},{6,4},{7,5},{8,10},{9,11},{10,... | collective-permute-start | bytes 6291464 | tf_op jit(solution)/shard_map/ppermute | solution.py:409
  243.3 44.0 %collective-permute-start.10 = (bf16[256,4096]{1,0:T(8,128)(2,1)S(1)}, bf16[256,4096]{1,0:T(8,128)(2,1)}, u32[]{:S(2)}, u32[]{:S(2)}) collective-permute-start(bf16[256,4096]{1,0:T(8,128)(2,1)S(1)} %get-tuple-element.65.refs_0_), channel_id=1, source_target_pairs={{0,1},{1,0},{2,3},{3,2},{4,5},{5,4},{6,7},{7,6},{8,9},{9,8},{10,11... | collective-permute-start | bytes 6291464 | tf_op jit(solution)/shard_map/ppermute | solution.py:404
  287.3 58.3 %copy-start.6 = (bf16[256,4096]{1,0:T(8,128)(2,1)}, bf16[256,4096]{1,0:T(8,128)(2,1)S(1)}, u32[]{:S(2)}) copy-start(bf16[256,4096]{1,0:T(8,128)(2,1)S(1)} %get-tuple-element.77.refs_0_) | copy-start | bytes 6291460
  287.3 58.6 %collective-permute-start.19 = (bf16[256,4096]{1,0:T(8,128)(2,1)S(1)}, bf16[256,4096]{1,0:T(8,128)(2,1)}, u32[]{:S(2)}, u32[]{:S(2)}) collective-permute-start(bf16[256,4096]{1,0:T(8,128)(2,1)S(1)} %get-tuple-element.77.refs_0_), channel_id=1, source_target_pairs={{0,1},{1,0},{2,3},{3,2},{4,5},{5,4},{6,7},{7,6},{8,9},{9,8},{10,11... | collective-permute-start | bytes 6291464 | tf_op jit(solution)/shard_map/ppermute | solution.py:404
  345.6 58.5 %copy-start.32 = (bf16[256,4096]{1,0:T(8,128)(2,1)S(1)}, bf16[256,4096]{1,0:T(8,128)(2,1)}, u32[]{:S(2)}) copy-start(bf16[256,4096]{1,0:T(8,128)(2,1)} %get-tuple-element.66) | copy-start | bytes 6291460
  345.6 58.5 %collective-permute-start.11 = (bf16[256,4096]{1,0:T(8,128)(2,1)}, bf16[256,4096]{1,0:T(8,128)(2,1)}, u32[]{:S(2)}, u32[]{:S(2)}) collective-permute-start(bf16[256,4096]{1,0:T(8,128)(2,1)} %get-tuple-element.67), channel_id=1, source_target_pairs={{0,1},{1,0},{2,3},{3,2},{4,5},{5,4},{6,7},{7,6},{8,9},{9,8},{10,11... | collective-permute-start | bytes 6291464 | tf_op jit(solution)/shard_map/ppermute | solution.py:407
  403.8 4.4 collective-permute-start.20
  406.6 48.6 %collective-permute-start.12 = (bf16[256,4096]{1,0:T(8,128)(2,1)S(1)}, bf16[256,4096]{1,0:T(8,128)(2,1)S(1)}, u32[]{:S(2)}, u32[]{:S(2)}) collective-permute-start(bf16[256,4096]{1,0:T(8,128)(2,1)S(1)} %add_convert_fusion.6.s_ref), channel_id=1, source_target_pairs={{0,2},{1,3},{2,0},{3,1},{4,6},{5,7},{6,4},{7,5},{8,10},{9,11},{10,... | collective-permute-start | bytes 6291464 | tf_op jit(solution)/shard_map/ppermute | solution.py:409
  408.2 47.0 %copy-start.13 = (bf16[256,4096]{1,0:T(8,128)(2,1)S(1)}, bf16[256,4096]{1,0:T(8,128)(2,1)}, u32[]{:S(2)}) copy-start(bf16[256,4096]{1,0:T(8,128)(2,1)} %copy-done.12) | copy-start | bytes 6291460
  409.0 90.4 %collective-permute-start.21 = (bf16[256,4096]{1,0:T(8,128)(2,1)S(1)}, bf16[256,4096]{1,0:T(8,128)(2,1)S(1)}, u32[]{:S(2)}, u32[]{:S(2)}) collective-permute-start(bf16[256,4096]{1,0:T(8,128)(2,1)S(1)} %add_convert_fusion.4.s_ref), channel_id=1, source_target_pairs={{0,2},{1,3},{2,0},{3,1},{4,6},{5,7},{6,4},{7,5},{8,10},{9,11},{10,... | collective-permute-start | bytes 6291464 | tf_op jit(solution)/shard_map/ppermute | solution.py:409
  455.2 44.2 %copy-start.11 = (bf16[256,4096]{1,0:T(8,128)(2,1)S(1)}, bf16[256,4096]{1,0:T(8,128)(2,1)}, u32[]{:S(2)}) copy-start(bf16[256,4096]{1,0:T(8,128)(2,1)} %copy-done.10) | copy-start | bytes 6291460
  456.9 60.0 %collective-permute-start.13 = (bf16[256,4096]{1,0:T(8,128)(2,1)S(1)}, bf16[256,4096]{1,0:T(8,128)(2,1)S(1)}, u32[]{:S(2)}, u32[]{:S(2)}) collective-permute-start(bf16[256,4096]{1,0:T(8,128)(2,1)S(1)} %get-tuple-element.69.refs_0_), channel_id=1, source_target_pairs={{0,1},{1,0},{2,3},{3,2},{4,5},{5,4},{6,7},{7,6},{8,9},{9,8},{10,11... | collective-permute-start | bytes 6291464 | tf_op jit(solution)/shard_map/ppermute | solution.py:404
  502.3 21.9 %collective-permute-start.22 = (bf16[256,4096]{1,0:T(8,128)(2,1)}, bf16[256,4096]{1,0:T(8,128)(2,1)}, u32[]{:S(2)}, u32[]{:S(2)}) collective-permute-start(bf16[256,4096]{1,0:T(8,128)(2,1)} %get-tuple-element.80.refs_0_), channel_id=1, source_target_pairs={{0,1},{1,0},{2,3},{3,2},{4,5},{5,4},{6,7},{7,6},{8,9},{9,8},{10,11... | collective-permute-start | bytes 6291464 | tf_op jit(solution)/shard_map/ppermute | solution.py:404
  520.2 25.9 %collective-permute-start.14 = (bf16[512,256]{1,0:T(8,128)(2,1)S(1)}, bf16[512,256]{1,0:T(8,128)(2,1)S(1)}, u32[]{:S(2)}, u32[]{:S(2)}) collective-permute-start(bf16[512,256]{1,0:T(8,128)(2,1)S(1)} %get-tuple-element.72.refs_2_), channel_id=1, source_target_pairs={{0,4},{4,8},{8,12},{1,5},{5,9},{9,13},{2,6},{6,10},{10,14},{3,7},{... | collective-permute-start | bytes 786440 | tf_op jit(solution)/shard_map/ppermute | solution.py:428
  522.1 24.7 %collective-permute-start.15 = (bf16[512,256]{1,0:T(8,128)(2,1)S(1)}, bf16[512,256]{1,0:T(8,128)(2,1)S(1)}, u32[]{:S(2)}, u32[]{:S(2)}) collective-permute-start(bf16[512,256]{1,0:T(8,128)(2,1)S(1)} %get-tuple-element.72.refs_2_), channel_id=1, source_target_pairs={{0,8},{4,12},{1,9},{5,13},{2,10},{6,14},{3,11},{7,15},{16,24},{20,... | collective-permute-start | bytes 786440 | tf_op jit(solution)/shard_map/ppermute | solution.py:428
  523.4 33.0 %collective-permute-start.16 = (bf16[512,256]{1,0:T(8,128)(2,1)S(1)}, bf16[512,256]{1,0:T(8,128)(2,1)S(1)}, u32[]{:S(2)}, u32[]{:S(2)}) collective-permute-start(bf16[512,256]{1,0:T(8,128)(2,1)S(1)} %get-tuple-element.72.refs_2_), channel_id=1, source_target_pairs={{0,12},{1,13},{2,14},{3,15},{16,28},{17,29},{18,30},{19,31}} | collective-permute-start | bytes 786440 | tf_op jit(solution)/shard_map/ppermute | solution.py:428
  529.3 33.2 %collective-permute-start.23 = (bf16[512,256]{1,0:T(8,128)(2,1)S(1)}, bf16[512,256]{1,0:T(8,128)(2,1)}, u32[]{:S(2)}, u32[]{:S(2)}) collective-permute-start(bf16[512,256]{1,0:T(8,128)(2,1)S(1)} %get-tuple-element.81.refs_6_), channel_id=1, source_target_pairs={{0,4},{4,8},{8,12},{1,5},{5,9},{9,13},{2,6},{6,10},{10,14},{3,7},{... | collective-permute-start | bytes 786440 | tf_op jit(solution)/shard_map/ppermute | solution.py:428
  531.2 48.1 %collective-permute-start.24 = (bf16[512,256]{1,0:T(8,128)(2,1)S(1)}, bf16[512,256]{1,0:T(8,128)(2,1)}, u32[]{:S(2)}, u32[]{:S(2)}) collective-permute-start(bf16[512,256]{1,0:T(8,128)(2,1)S(1)} %get-tuple-element.81.refs_6_), channel_id=1, source_target_pairs={{0,8},{4,12},{1,9},{5,13},{2,10},{6,14},{3,11},{7,15},{16,24},{20,... | collective-permute-start | bytes 786440 | tf_op jit(solution)/shard_map/ppermute | solution.py:428
  546.1 35.2 %collective-permute-start.25 = (bf16[512,256]{1,0:T(8,128)(2,1)S(1)}, bf16[512,256]{1,0:T(8,128)(2,1)S(1)}, u32[]{:S(2)}, u32[]{:S(2)}) collective-permute-start(bf16[512,256]{1,0:T(8,128)(2,1)S(1)} %get-tuple-element.81.refs_6_), channel_id=1, source_target_pairs={{0,12},{1,13},{2,14},{3,15},{16,28},{17,29},{18,30},{19,31}} | collective-permute-start | bytes 786440 | tf_op jit(solution)/shard_map/ppermute | solution.py:428
  546.8 39.3 %collective-permute-start.26 = (bf16[512,256]{1,0:T(8,128)(2,1)S(1)}, bf16[512,256]{1,0:T(8,128)(2,1)S(1)}, u32[]{:S(2)}, u32[]{:S(2)}) collective-permute-start(bf16[512,256]{1,0:T(8,128)(2,1)S(1)} %get-tuple-element.82.refs_2_), channel_id=1, source_target_pairs={{0,4},{4,8},{8,12},{1,5},{5,9},{9,13},{2,6},{6,10},{10,14},{3,7},{... | collective-permute-start | bytes 786440 | tf_op jit(solution)/shard_map/ppermute | solution.py:428
  557.1 44.7 %collective-permute-start.27 = (bf16[512,256]{1,0:T(8,128)(2,1)S(1)}, bf16[512,256]{1,0:T(8,128)(2,1)S(1)}, u32[]{:S(2)}, u32[]{:S(2)}) collective-permute-start(bf16[512,256]{1,0:T(8,128)(2,1)S(1)} %get-tuple-element.82.refs_2_), channel_id=1, source_target_pairs={{0,8},{4,12},{1,9},{5,13},{2,10},{6,14},{3,11},{7,15},{16,24},{20,... | collective-permute-start | bytes 786440 | tf_op jit(solution)/shard_map/ppermute | solution.py:428
  562.5 39.4 %collective-permute-start.28 = (bf16[512,256]{1,0:T(8,128)(2,1)S(1)}, bf16[512,256]{1,0:T(8,128)(2,1)S(1)}, u32[]{:S(2)}, u32[]{:S(2)}) collective-permute-start(bf16[512,256]{1,0:T(8,128)(2,1)S(1)} %get-tuple-element.82.refs_2_), channel_id=1, source_target_pairs={{0,12},{1,13},{2,14},{3,15},{16,28},{17,29},{18,30},{19,31}} | collective-permute-start | bytes 786440 | tf_op jit(solution)/shard_map/ppermute | solution.py:428
  579.4 28.1 %collective-permute-start.29 = (bf16[512,256]{1,0:T(8,128)(2,1)S(1)}, bf16[512,256]{1,0:T(8,128)(2,1)S(1)}, u32[]{:S(2)}, u32[]{:S(2)}) collective-permute-start(bf16[512,256]{1,0:T(8,128)(2,1)S(1)} %get-tuple-element.83.refs_6_), channel_id=1, source_target_pairs={{0,4},{4,8},{8,12},{1,5},{5,9},{9,13},{2,6},{6,10},{10,14},{3,7},{... | collective-permute-start | bytes 786440 | tf_op jit(solution)/shard_map/ppermute | solution.py:428
  581.3 31.6 %collective-permute-start.30 = (bf16[512,256]{1,0:T(8,128)(2,1)S(1)}, bf16[512,256]{1,0:T(8,128)(2,1)S(1)}, u32[]{:S(2)}, u32[]{:S(2)}) collective-permute-start(bf16[512,256]{1,0:T(8,128)(2,1)S(1)} %get-tuple-element.83.refs_6_), channel_id=1, source_target_pairs={{0,8},{4,12},{1,9},{5,13},{2,10},{6,14},{3,11},{7,15},{16,24},{20,... | collective-permute-start | bytes 786440 | tf_op jit(solution)/shard_map/ppermute | solution.py:428
  586.1 26.8 %collective-permute-start.31 = (bf16[512,256]{1,0:T(8,128)(2,1)S(1)}, bf16[512,256]{1,0:T(8,128)(2,1)S(1)}, u32[]{:S(2)}, u32[]{:S(2)}) collective-permute-start(bf16[512,256]{1,0:T(8,128)(2,1)S(1)} %get-tuple-element.83.refs_6_), channel_id=1, source_target_pairs={{0,12},{1,13},{2,14},{3,15},{16,28},{17,29},{18,30},{19,31}} | collective-permute-start | bytes 786440 | tf_op jit(solution)/shard_map/ppermute | solution.py:428
  632.4 32.4 %collective-permute-start.37 = (bf16[256,4096]{1,0:T(8,128)(2,1)S(1)}, bf16[256,4096]{1,0:T(8,128)(2,1)S(1)}, u32[]{:S(2)}, u32[]{:S(2)}) collective-permute-start(bf16[256,4096]{1,0:T(8,128)(2,1)S(1)} %get-tuple-element.92), channel_id=1, source_target_pairs={{0,1},{1,0},{2,3},{3,2},{4,5},{5,4},{6,7},{7,6},{8,9},{9,8},{10,11... | collective-permute-start | bytes 6291464 | tf_op jit(solution)/shard_map/ppermute | solution.py:407
  664.2 4.3 collective-permute-start.32
  665.6 48.6 %collective-permute-start.38 = (bf16[256,4096]{1,0:T(8,128)(2,1)S(1)}, bf16[256,4096]{1,0:T(8,128)(2,1)S(1)}, u32[]{:S(2)}, u32[]{:S(2)}) collective-permute-start(bf16[256,4096]{1,0:T(8,128)(2,1)S(1)} %add_convert_fusion.1.s_ref), channel_id=1, source_target_pairs={{0,2},{1,3},{2,0},{3,1},{4,6},{5,7},{6,4},{7,5},{8,10},{9,11},{10,... | collective-permute-start | bytes 6291464 | tf_op jit(solution)/shard_map/ppermute | solution.py:409
  669.4 88.8 %collective-permute-start.33 = (bf16[256,4096]{1,0:T(8,128)(2,1)S(1)}, bf16[256,4096]{1,0:T(8,128)(2,1)S(1)}, u32[]{:S(2)}, u32[]{:S(2)}) collective-permute-start(bf16[256,4096]{1,0:T(8,128)(2,1)S(1)} %add_convert_fusion.3.s_ref), channel_id=1, source_target_pairs={{0,2},{1,3},{2,0},{3,1},{4,6},{5,7},{6,4},{7,5},{8,10},{9,11},{10,... | collective-permute-start | bytes 6291464 | tf_op jit(solution)/shard_map/ppermute | solution.py:409
  715.9 45.3 %collective-permute-start.39 = (bf16[256,4096]{1,0:T(8,128)(2,1)S(1)}, bf16[256,4096]{1,0:T(8,128)(2,1)}, u32[]{:S(2)}, u32[]{:S(2)}) collective-permute-start(bf16[256,4096]{1,0:T(8,128)(2,1)S(1)} %get-tuple-element.94.refs_0_), channel_id=1, source_target_pairs={{0,1},{1,0},{2,3},{3,2},{4,5},{5,4},{6,7},{7,6},{8,9},{9,8},{10,11... | collective-permute-start | bytes 6291464 | tf_op jit(solution)/shard_map/ppermute | solution.py:404
  761.2 58.3 %copy-start.7 = (bf16[256,4096]{1,0:T(8,128)(2,1)}, bf16[256,4096]{1,0:T(8,128)(2,1)S(1)}, u32[]{:S(2)}) copy-start(bf16[256,4096]{1,0:T(8,128)(2,1)S(1)} %get-tuple-element.87.refs_0_) | copy-start | bytes 6291460
  761.2 58.4 %collective-permute-start.34 = (bf16[256,4096]{1,0:T(8,128)(2,1)S(1)}, bf16[256,4096]{1,0:T(8,128)(2,1)}, u32[]{:S(2)}, u32[]{:S(2)}) collective-permute-start(bf16[256,4096]{1,0:T(8,128)(2,1)S(1)} %get-tuple-element.87.refs_0_), channel_id=1, source_target_pairs={{0,1},{1,0},{2,3},{3,2},{4,5},{5,4},{6,7},{7,6},{8,9},{9,8},{10,11... | collective-permute-start | bytes 6291464 | tf_op jit(solution)/shard_map/ppermute | solution.py:404
  819.5 58.6 %copy-start.34 = (bf16[256,4096]{1,0:T(8,128)(2,1)S(1)}, bf16[256,4096]{1,0:T(8,128)(2,1)}, u32[]{:S(2)}) copy-start(bf16[256,4096]{1,0:T(8,128)(2,1)} %get-tuple-element.95) | copy-start | bytes 6291460
  819.5 58.6 %collective-permute-start.40 = (bf16[256,4096]{1,0:T(8,128)(2,1)}, bf16[256,4096]{1,0:T(8,128)(2,1)}, u32[]{:S(2)}, u32[]{:S(2)}) collective-permute-start(bf16[256,4096]{1,0:T(8,128)(2,1)} %get-tuple-element.96), channel_id=1, source_target_pairs={{0,1},{1,0},{2,3},{3,2},{4,5},{5,4},{6,7},{7,6},{8,9},{9,8},{10,11... | collective-permute-start | bytes 6291464 | tf_op jit(solution)/shard_map/ppermute | solution.py:412
  877.6 4.5 collective-permute-start.35
  880.6 26.1 %collective-permute-start.41 = (bf16[128,4096]{1,0:T(8,128)(2,1)S(1)}, bf16[128,4096]{1,0:T(8,128)(2,1)S(1)}, u32[]{:S(2)}, u32[]{:S(2)}) collective-permute-start(bf16[128,4096]{1,0:T(8,128)(2,1)S(1)} %slice.73), channel_id=1, source_target_pairs={{0,2},{1,3},{2,0},{3,1},{4,6},{5,7},{6,4},{7,5},{8,10},{9,11},{10,... | collective-permute-start | bytes 3145736 | tf_op jit(solution)/shard_map/ppermute | solution.py:414
  883.0 45.3 %collective-permute-start.36 = (bf16[128,4096]{1,0:T(8,128)(2,1)S(1)}, bf16[128,4096]{1,0:T(8,128)(2,1)S(1)}, u32[]{:S(2)}, u32[]{:S(2)}) collective-permute-start(bf16[128,4096]{1,0:T(8,128)(2,1)S(1)} %slice.71), channel_id=1, source_target_pairs={{0,2},{1,3},{2,0},{3,1},{4,6},{5,7},{6,4},{7,5},{8,10},{9,11},{10,... | collective-permute-start | bytes 3145736 | tf_op jit(solution)/shard_map/ppermute | solution.py:414
  (31 other events, 466.3 us)

commit v2 on v1

--- a/solution.py
+++ b/solution.py
@@ -94,12 +94,16 @@
         o_ref[:, cols] = rotate(t[:, cols], cos_ref[...], sin_ref[...])
 
 
-def kv_kernel(*refs):
+def kv_kernel(split, *refs):
     xs, (w_ref, cos_ref, sin_ref), os = refs[:2], refs[2:5], refs[5:]
     step = pl.program_id(0)
     x = jnp.concatenate([r[...] for r in xs], axis=0)
     t = jnp.dot(x, w_ref[...], preferred_element_type=jnp.float32).astype(jnp.bfloat16)
     k = rotate(t[:, :HEAD], cos_ref[...], sin_ref[...])
+    if not split:
+        os[0][:, :HEAD] = k
+        os[0][:, HEAD:] = t[:, HEAD:]
+        return
     for h, o in enumerate(os):
         @pl.when(step == h)
         def _():
@@ -151,11 +155,10 @@
     )(a, b, gain.astype(jnp.float32)[None])
 
 
-def flash_kernel(chunk, windowed, n_rel, part, group, nh, scale, *refs):
+def flash_kernel(cols, chunk, windowed, n_rel, part, group, nh, scale, *refs):
     sc_ref, q_ref = refs[:2]
-    count = CHUNKS * n_rel
-    kv_in = refs[2:2 + nh * count]
-    o_ref, kv_ref, m_ref, l_ref, acc_ref, sem = refs[2 + nh * count:]
+    kv_in = refs[2:2 + len(cols)]
+    o_ref, kv_ref, m_ref, l_ref, acc_ref, sem = refs[2 + len(cols):]
     keys = 512 if windowed else 1024
     tile = pl.program_id(0)
     here, mine, cut1, cut2 = sc_ref[0], sc_ref[1], sc_ref[2], sc_ref[3]
@@ -170,7 +173,7 @@
                     i = (g * CHUNKS + c) * n_rel + rel
                     for slot, flip in enumerate((0, 2, 1, 3)):
                         dst = pl.multiple_of(rel * 4 * rows + (mine ^ flip) * rows + c * part, part)
-                        copies.append(pltpu.make_async_copy(kv_in[i].at[pl.ds(slot * part, part)], kv_ref.at[g, pl.ds(dst, part)], sem.at[4 * i + slot]))
+                        copies.append(pltpu.make_async_copy(kv_in[i].at[pl.ds(slot * part, part), pl.ds(cols[i] * 2 * HEAD, 2 * HEAD)], kv_ref.at[g, pl.ds(dst, part)], sem.at[4 * i + slot]))
         for c in copies:
             c.start()
         for c in copies:
@@ -235,13 +238,14 @@
     rows = q.shape[0]
     nh = len(kv_pieces)
     width = q.shape[1] * nh // kv_heads
-    flat = [p for pieces in kv_pieces for p in pieces]
+    flat = [p[0] for pieces in kv_pieces for p in pieces]
+    cols = tuple(p[1] for pieces in kv_pieces for p in pieces)
     n_rel = len(kv_pieces[0]) // CHUNKS
     group = width // HEAD // nh
     part = rows // 4
     state = pltpu.VMEM((2, nh * group * part // 2, HEAD), jnp.float32)
     return pl.pallas_call(
-        functools.partial(flash_kernel, chunk, windowed, n_rel, part, group, nh, HEAD ** -0.5 * LOG2E),
+        functools.partial(flash_kernel, cols, chunk, windowed, n_rel, part, group, nh, HEAD ** -0.5 * LOG2E),
         grid_spec=pltpu.PrefetchScalarGridSpec(
             num_scalar_prefetch=1,
             grid=(4,),
@@ -364,28 +368,34 @@
         rows = x.shape[0]
         part = rows // CHUNKS
         group_rows = rows * tp_size
-        order = [tp_idx, tp_idx ^ 2, tp_idx ^ 1, tp_idx ^ 3]
         which = tp_idx.astype(jnp.int32)[None]
 
-        ids = lax.all_gather(jnp.stack([segment_ids, positions]), ("sp", "tp"))
-        x, ids = lax.optimization_barrier((x, ids))
-        own = [x[c * part:(c + 1) * part] for c in range(CHUNKS)]
+        ids = jnp.stack([segment_ids, positions])
+        far = lax.ppermute(ids, "tp", across)
+        both = jnp.stack([ids, far])
+        beside = lax.ppermute(both, "tp", near)
+        ids = jnp.concatenate([both, beside])
+        own, others = [x[c * part:(c + 1) * part] for c in range(CHUNKS)], []
+        for c in range(CHUNKS):
+            others.append(lax.ppermute(own[c], "tp", across))
         resid, normed = [], []
         for c in range(CHUNKS):
-            other = lax.ppermute(own[c], "tp", across)
-            pair = first_norm(own[c], other, g_attn[0])
+            pair = first_norm(own[c], others[c], g_attn[0])
             resid.append(pair[0])
             normed.append(pair[1])
 
-        seg_all = ids[:, 0].reshape(-1)
-        starts = [jnp.sum((seg_all < s).astype(jnp.int32)) for s in (1, 2)]
-        pos_here = lax.dynamic_slice_in_dim(ids[:, 1], sp_idx * tp_size, tp_size, 0)
+        before = jnp.stack([jnp.sum((ids[:, 0] < s).astype(jnp.int32)) for s in (1, 2)])
+        before = jnp.broadcast_to(before[:, None], (2, HEAD))
+        for hop in (1, 2):
+            far = lax.ppermute(before, "sp", [(z, z ^ hop) for z in range(sp_size)])
+            before = before + far
+        starts = [before[0, 0], before[1, 0]]
         half = HEAD // 2
         inv_freq = ROPE_BASE ** (-jnp.arange(half, dtype=jnp.float32) / half)
         inv_freq = jnp.concatenate([inv_freq, inv_freq])
         sign = jnp.where(jnp.arange(HEAD) < half, -1.0, 1.0)
         cos_t, sin_t = [], []
-        pos_rel = jnp.concatenate([lax.dynamic_slice_in_dim(pos_here, o, 1, 0) for o in order])
+        pos_rel = ids[:, 1]
         for c in range(CHUNKS):
             pos = pos_rel[:, c * part:(c + 1) * part].reshape(-1)
             angles = pos.astype(jnp.float32)[:, None] * inv_freq[None, :]
@@ -421,11 +431,14 @@
             q, kv = [], [[] for _ in range(kv_heads)]
             for c in range(CHUNKS):
                 full = share(normed[c])
-                mine = project(kv_kernel, full, wkv_l[layer], cos_t[c], sin_t[c], kv_heads)
-                for h in range(kv_heads):
-                    kv[h].append(mine[h])
+                split = not windowed and c == CHUNKS - 1
+                mine = project(functools.partial(kv_kernel, split), full, wkv_l[layer], cos_t[c], sin_t[c], kv_heads if split else 1)
+                for h, piece in enumerate(mine if split else [mine]):
+                    got = [piece]
                     for s in range(1, shifts + 1):
-                        kv[h].append(lax.ppermute(mine[h], "sp", [(z, z + s) for z in range(sp_size - s)]))
+                        got.append(lax.ppermute(piece, "sp", [(z, z + s) for z in range(sp_size - s)]))
+                    for g in [h] if split else range(kv_heads):
+                        kv[g] += [(v, 0 if split else g) for v in got]
                 q.append(project(q_kernel, full, wq_l[layer], cos_t[c], sin_t[c], 1))
             for c in range(CHUNKS):
                 mixed = []

time: 939 us -> 933 us (level)
  the two profiles are of different devices: /device:TPU:10 before, /device:TPU:18 now
where the time goes in v2:
time: 933 us; the launch traced here: 925 us
  Pallas kernels  429 us (46%)
  waiting for transfers between devices  408 us (44%)
  starting transfers between devices  39.9 us (4%)
  local copies, waits for them, and re-layouts  28.1 us (3%)
  other arithmetic  19.2 us (2%)
    ppermute x6, waiting for transfers between devices, exchange(): return (s, lax.ppermute(s, 'tp', across))  258 us
    pallas_call x4, Pallas kernels, mlp(): pl.pallas_call(mlp_kernel, grid=(ff // bf,), in_specs=[pl.BlockSpec((part...  232 us
    pallas_call x6, Pallas kernels, flash(): pl.pallas_call(functools.partial(flash_kernel, cols, chunk, windowed, n_r...  69.8 us
    ppermute x11, waiting for transfers between devices, local_fn(): lax.ppermute(piece, 'sp', [(z, z + s) for z in range(sp_size - s)])  60.9 us
    pallas_call x8, Pallas kernels, project(): pl.pallas_call(kernel, grid=(n // bn,), in_specs=[pl.BlockSpec(b.shape, l...  51.2 us
    ppermute x2, waiting for transfers between devices, exchange_last(): r = lax.ppermute(s[part:], 'tp', across)  43.2 us
    ppermute x2, waiting for transfers between devices, local_fn(): others.append(lax.ppermute(own[c], 'tp', across))  38.6 us
    pallas_call x2, Pallas kernels, relayout(): pl.pallas_call(relayout_kernel, grid_spec=pltpu.PrefetchScalarGridSpec(nu...  29.1 us
  transfers between devices with their start and end apart: 41, of which 18 were waited for; matrix products, arithmetic and copies ran while one was open for 2% of the time, Pallas kernels for 42%

profile of v2, /device:TPU:18, one launch (start us, length us, event | category | flops | bytes accessed | tf_op | source)
XLA Modules:
  0.0 925.2 jit_solution(264647589735667291)
XLA Ops:
  5.4 22.5 %collective-permute-done.7.b_ref = bf16[128,4096]{1,0:T(8,128)(2,1)} collective-permute-done((bf16[128,4096]{1,0:T(8,128)(2,1)S(1)}, bf16[128,4096]{1,0:T(8,128)(2,1)}, u32[]{:S(2)}, u32[]{:S(2)}) %collective-permute-start.7) | collective-permute-done | bytes 1048608 | tf_op jit(solution)/shard_map/ppermute | solution.py:380
  27.9 3.8 first_norm.3
  33.1 16.1 %collective-permute-done.b_ref = bf16[128,4096]{1,0:T(8,128)(2,1)S(1)} collective-permute-done((bf16[128,4096]{1,0:T(8,128)(2,1)S(1)}, bf16[128,4096]{1,0:T(8,128)(2,1)S(1)}, u32[]{:S(2)}, u32[]{:S(2)}) %collective-permute-start) | collective-permute-done | bytes 1048608 | tf_op jit(solution)/shard_map/ppermute | solution.py:380
  51.4 2.6 first_norm.2
  54.0 14.5 %relayout.2 = (bf16[4096,1024]{1,0:T(8,128)(2,1)S(1)}, bf16[4096,512]{1,0:T(8,128)(2,1)S(1)}) custom-call(s32[1]{0:T(128)} %bitcast.1.sc_ref, bf16[2,4096,8,128]{3,2,1,0:T(8,128)(2,1)} %wq_ref.3, bf16[2,4096,8,128]{3,2,1,0:T(8,128)(2,1)} %wk_ref.3, bf16[2,4096,8,128]{3,2,1,0:T(8,128)(2,1)} %wv_ref.3), custom_call_target="tpu_custom_call" | custom-call | flops 10000000000 | bytes 33554432 | tf_op jit(solution)/shard_map/relayout/pallas_call | solution.py:41
  70.6 3.3 copy-done.23
  87.9 5.2 shard_map.119.refs_2_.refs_6_
  93.1 3.5 collective-permute-start.6
  96.6 5.1 shard_map.120.refs_4_.refs_8_
  105.6 3.4 copy-done.24
  109.0 8.5 shard_map.118.refs_1_
  118.1 12.0 %flash.6.refs_0_ = bf16[512,1024]{1,0:T(8,128)(2,1)S(1)} custom-call(s32[4]{0:T(128)S(1)} %pad_add_fusion.4.refs_0_, bf16[512,1024]{1,0:T(8,128)(2,1)S(1)} %shard_map.118.refs_1_, bf16[512,512]{1,0:T(8,128)(2,1)S(1)} %shard_map.119.refs_2_.refs_6_, bf16[512,512]{1,0:T(8,128)(2,1)S(1)} %collective-permute-done.6.refs_3_.refs_7_, ...), custom_call_target="tpu_custom_call" | custom-call | flops 10000000000 | bytes 2097152 | tf_op jit(solution)/shard_map/flash/pallas_call | solution.py:247
  130.1 7.2 out_proj.4
  137.4 3.4 copy-done.25
  140.8 8.5 shard_map.123.refs_1_
  149.3 10.1 %flash.7.refs_0_ = bf16[512,1024]{1,0:T(8,128)(2,1)S(1)} custom-call(s32[4]{0:T(128)S(1)} %pad_add_fusion.4.refs_0_, bf16[512,1024]{1,0:T(8,128)(2,1)S(1)} %shard_map.123.refs_1_, bf16[512,512]{1,0:T(8,128)(2,1)S(1)} %shard_map.119.refs_2_.refs_6_, bf16[512,512]{1,0:T(8,128)(2,1)S(1)} %collective-permute-done.6.refs_3_.refs_7_, ...), custom_call_target="tpu_custom_call" | custom-call | flops 10000000000 | bytes 2097152 | tf_op jit(solution)/shard_map/flash/pallas_call | solution.py:247
  159.4 7.2 out_proj.5
  167.2 2.4 add_convert_fusion.7.s_ref
  173.3 44.8 %collective-permute-done.11.r_ref = bf16[256,4096]{1,0:T(8,128)(2,1)S(1)} collective-permute-done((bf16[256,4096]{1,0:T(8,128)(2,1)S(1)}, bf16[256,4096]{1,0:T(8,128)(2,1)S(1)}, u32[]{:S(2)}, u32[]{:S(2)}) %collective-permute-start.11) | collective-permute-done | bytes 2097184 | tf_op jit(solution)/shard_map/ppermute | solution.py:419
  219.9 42.2 %collective-permute-done.20.r_ref = bf16[256,4096]{1,0:T(8,128)(2,1)S(1)} collective-permute-done((bf16[256,4096]{1,0:T(8,128)(2,1)S(1)}, bf16[256,4096]{1,0:T(8,128)(2,1)S(1)}, u32[]{:S(2)}, u32[]{:S(2)}) %collective-permute-start.20) | collective-permute-done | bytes 2097184 | tf_op jit(solution)/shard_map/ppermute | solution.py:419
  265.2 58.3 %mlp.4 = (bf16[256,4096]{1,0:T(8,128)(2,1)}, bf16[256,4096]{1,0:T(8,128)(2,1)}) custom-call(bf16[256,4096]{1,0:T(8,128)(2,1)} %copy-done.7, bf16[256,4096]{1,0:T(8,128)(2,1)} %collective-permute-done.12.refs_1_, bf16[2,4096,3584]{2,1,0:T(8,128)(2,1)} %refs_2_.7, bf16[2,4096,3584]{2,1,0:T(8,128)(2,1)} %refs_3_.7, bf16[2,3584,4096]{2,1,0:T(8,128)(2,1)} %refs_4_.7), custom_call_target="tpu_custom_call" | custom-call | flops 45097156608 | bytes 88080384 | tf_op jit(solution)/shard_map/mlp/pallas_call | solution.py:339
  323.8 57.8 %mlp.5 = (bf16[256,4096]{1,0:T(8,128)(2,1)}, bf16[256,4096]{1,0:T(8,128)(2,1)}) custom-call(bf16[256,4096]{1,0:T(8,128)(2,1)} %copy-done.9, bf16[256,4096]{1,0:T(8,128)(2,1)} %collective-permute-done.21.refs_1_, bf16[2,4096,3584]{2,1,0:T(8,128)(2,1)} %refs_2_.7, bf16[2,4096,3584]{2,1,0:T(8,128)(2,1)} %refs_3_.7, bf16[2,3584,4096]{2,1,0:T(8,128)(2,1)} %refs_4_.7), custom_call_target="tpu_custom_call" | custom-call | flops 45097156608 | bytes 88080384 | tf_op jit(solution)/shard_map/mlp/pallas_call | solution.py:339
  381.9 2.5 add_convert_fusion.6.s_ref
  388.5 44.6 %collective-permute-done.14.r_ref = bf16[256,4096]{1,0:T(8,128)(2,1)S(1)} collective-permute-done((bf16[256,4096]{1,0:T(8,128)(2,1)S(1)}, bf16[256,4096]{1,0:T(8,128)(2,1)S(1)}, u32[]{:S(2)}, u32[]{:S(2)}) %collective-permute-start.14) | collective-permute-done | bytes 2097184 | tf_op jit(solution)/shard_map/ppermute | solution.py:419
  433.0 2.8 residual_norm.7
  435.9 41.5 %collective-permute-done.23.r_ref = bf16[256,4096]{1,0:T(8,128)(2,1)S(1)} collective-permute-done((bf16[256,4096]{1,0:T(8,128)(2,1)S(1)}, bf16[256,4096]{1,0:T(8,128)(2,1)S(1)}, u32[]{:S(2)}, u32[]{:S(2)}) %collective-permute-start.23) | collective-permute-done | bytes 2097184 | tf_op jit(solution)/shard_map/ppermute | solution.py:419
  479.1 14.6 %relayout.3 = (bf16[4096,1024]{1,0:T(8,128)(2,1)S(1)}, bf16[4096,512]{1,0:T(8,128)(2,1)S(1)}) custom-call(s32[1]{0:T(128)} %bitcast.1.sc_ref, bf16[2,4096,8,128]{3,2,1,0:T(8,128)(2,1)} %wq_ref.3, bf16[2,4096,8,128]{3,2,1,0:T(8,128)(2,1)} %wk_ref.3, bf16[2,4096,8,128]{3,2,1,0:T(8,128)(2,1)} %wv_ref.3), custom_call_target="tpu_custom_call" | custom-call | flops 10000000000 | bytes 33554432 | tf_op jit(solution)/shard_map/relayout/pallas_call | solution.py:41
  493.7 3.3 copy-done.26
  497.1 5.1 shard_map.122.refs_2_
  502.2 2.3 collective-permute-start.16
  507.4 3.8 shard_map.124
  514.4 6.6 shard_map.125.refs_1_
  521.9 53.0 %collective-permute-done.25.refs_7_ = bf16[512,256]{1,0:T(8,128)(2,1)S(1)} collective-permute-done((bf16[512,256]{1,0:T(8,128)(2,1)}, bf16[512,256]{1,0:T(8,128)(2,1)S(1)}, u32[]{:S(2)}, u32[]{:S(2)}) %collective-permute-start.25) | collective-permute-done | bytes 262176 | tf_op jit(solution)/shard_map/ppermute | solution.py:439
  576.4 8.5 shard_map.121.refs_1_
  588.9 11.1 %flash.10.refs_0_ = bf16[512,512]{1,0:T(8,128)(2,1)S(1)} custom-call(s32[4]{0:T(128)S(1)} %pad_add_fusion.4.refs_0_, bf16[512,1024]{1,0:T(8,128)(2,1)S(1)} %copy-done.31, bf16[512,512]{1,0:T(8,128)(2,1)S(1)} %shard_map.122.refs_2_, bf16[512,512]{1,0:T(8,128)(2,1)S(1)} %collective-permute-done.16.refs_3_, ...), custom_call_target="tpu_custom_call" | custom-call | flops 10000000000 | bytes 1048576 | tf_op jit(solution)/shard_map/flash/pallas_call | solution.py:247
  600.1 7.2 collective-permute-done.28.refs_7_
  607.3 11.0 %flash.11.refs_1_ = bf16[512,512]{1,0:T(8,128)(2,1)S(1)} custom-call(s32[4]{0:T(128)S(1)} %pad_add_fusion.4.refs_0_, bf16[512,1024]{1,0:T(8,128)(2,1)S(1)} %copy-done.31, bf16[512,512]{1,0:T(8,128)(2,1)S(1)} %shard_map.122.refs_2_, bf16[512,512]{1,0:T(8,128)(2,1)S(1)} %collective-permute-done.16.refs_3_, ...), custom_call_target="tpu_custom_call" | custom-call | flops 10000000000 | bytes 1048576 | tf_op jit(solution)/shard_map/flash/pallas_call | solution.py:247
  618.3 7.3 out_proj.7
  625.6 12.8 %flash.8.refs_0_ = bf16[512,512]{1,0:T(8,128)(2,1)S(1)} custom-call(s32[4]{0:T(128)S(1)} %pad_add_fusion.4.refs_0_, bf16[512,1024]{1,0:T(8,128)(2,1)S(1)} %shard_map.121.refs_1_, bf16[512,512]{1,0:T(8,128)(2,1)S(1)} %shard_map.122.refs_2_, bf16[512,512]{1,0:T(8,128)(2,1)S(1)} %collective-permute-done.16.refs_3_, ...), custom_call_target="tpu_custom_call" | custom-call | flops 10000000000 | bytes 1048576 | tf_op jit(solution)/shard_map/flash/pallas_call | solution.py:247
  638.4 12.9 %flash.9.refs_1_ = bf16[512,512]{1,0:T(8,128)(2,1)S(1)} custom-call(s32[4]{0:T(128)S(1)} %pad_add_fusion.4.refs_0_, bf16[512,1024]{1,0:T(8,128)(2,1)S(1)} %shard_map.121.refs_1_, bf16[512,512]{1,0:T(8,128)(2,1)S(1)} %shard_map.122.refs_2_, bf16[512,512]{1,0:T(8,128)(2,1)S(1)} %collective-permute-done.16.refs_3_, ...), custom_call_target="tpu_custom_call" | custom-call | flops 10000000000 | bytes 1048576 | tf_op jit(solution)/shard_map/flash/pallas_call | solution.py:247
  651.3 7.2 out_proj.6
  665.3 43.2 %collective-permute-done.37.r_ref = bf16[256,4096]{1,0:T(8,128)(2,1)S(1)} collective-permute-done((bf16[256,4096]{1,0:T(8,128)(2,1)S(1)}, bf16[256,4096]{1,0:T(8,128)(2,1)S(1)}, u32[]{:S(2)}, u32[]{:S(2)}) %collective-permute-start.37) | collective-permute-done | bytes 2097184 | tf_op jit(solution)/shard_map/ppermute | solution.py:419
  710.3 42.2 %collective-permute-done.32.r_ref = bf16[256,4096]{1,0:T(8,128)(2,1)S(1)} collective-permute-done((bf16[256,4096]{1,0:T(8,128)(2,1)S(1)}, bf16[256,4096]{1,0:T(8,128)(2,1)S(1)}, u32[]{:S(2)}, u32[]{:S(2)}) %collective-permute-start.32) | collective-permute-done | bytes 2097184 | tf_op jit(solution)/shard_map/ppermute | solution.py:419
  755.5 58.3 %mlp.7 = (bf16[256,4096]{1,0:T(8,128)(2,1)}, bf16[256,4096]{1,0:T(8,128)(2,1)}) custom-call(bf16[256,4096]{1,0:T(8,128)(2,1)} %copy-done.8, bf16[256,4096]{1,0:T(8,128)(2,1)} %collective-permute-done.38.refs_1_, bf16[2,4096,3584]{2,1,0:T(8,128)(2,1)} %refs_2_.7, bf16[2,4096,3584]{2,1,0:T(8,128)(2,1)} %refs_3_.7, bf16[2,3584,4096]{2,1,0:T(8,128)(2,1)} %refs_4_.7), custom_call_target="tpu_custom_call" | custom-call | flops 45097156608 | bytes 88080384 | tf_op jit(solution)/shard_map/mlp/pallas_call | solution.py:339
  814.0 58.0 %mlp.6 = (bf16[256,4096]{1,0:T(8,128)(2,1)}, bf16[256,4096]{1,0:T(8,128)(2,1)}) custom-call(bf16[256,4096]{1,0:T(8,128)(2,1)} %copy-done.10, bf16[256,4096]{1,0:T(8,128)(2,1)} %collective-permute-done.33.refs_1_, bf16[2,4096,3584]{2,1,0:T(8,128)(2,1)} %refs_2_.7, bf16[2,4096,3584]{2,1,0:T(8,128)(2,1)} %refs_3_.7, bf16[2,3584,4096]{2,1,0:T(8,128)(2,1)} %refs_4_.7), custom_call_target="tpu_custom_call" | custom-call | flops 45097156608 | bytes 88080384 | tf_op jit(solution)/shard_map/mlp/pallas_call | solution.py:339
  872.4 2.4 add_convert_fusion
  878.9 22.1 %collective-permute-done.40 = bf16[128,4096]{1,0:T(8,128)(2,1)S(1)} collective-permute-done((bf16[128,4096]{1,0:T(8,128)(2,1)S(1)}, bf16[128,4096]{1,0:T(8,128)(2,1)S(1)}, u32[]{:S(2)}, u32[]{:S(2)}) %collective-permute-start.40) | collective-permute-done | bytes 1048608 | tf_op jit(solution)/shard_map/ppermute | solution.py:424
  901.5 21.1 %collective-permute-done.35 = bf16[128,4096]{1,0:T(8,128)(2,1)S(1)} collective-permute-done((bf16[128,4096]{1,0:T(8,128)(2,1)S(1)}, bf16[128,4096]{1,0:T(8,128)(2,1)S(1)}, u32[]{:S(2)}, u32[]{:S(2)}) %collective-permute-start.35) | collective-permute-done | bytes 1048608 | tf_op jit(solution)/shard_map/ppermute | solution.py:424
  (178 shorter events, 76.1 us)
Async XLA Ops:
  1.7 26.2 %collective-permute-start.7 = (bf16[128,4096]{1,0:T(8,128)(2,1)S(1)}, bf16[128,4096]{1,0:T(8,128)(2,1)}, u32[]{:S(2)}, u32[]{:S(2)}) collective-permute-start(bf16[128,4096]{1,0:T(8,128)(2,1)S(1)} %get-tuple-element.84.a_ref), channel_id=1, source_target_pairs={{0,2},{1,3},{2,0},{3,1},{4,6},{5,7},{6,4},{7,5},{8,10},{9,11},{10,... | collective-permute-start | bytes 3145736 | tf_op jit(solution)/shard_map/ppermute | solution.py:380
  3.3 45.9 %collective-permute-start = (bf16[128,4096]{1,0:T(8,128)(2,1)S(1)}, bf16[128,4096]{1,0:T(8,128)(2,1)S(1)}, u32[]{:S(2)}, u32[]{:S(2)}) collective-permute-start(bf16[128,4096]{1,0:T(8,128)(2,1)S(1)} %get-tuple-element.83.a_ref), channel_id=1, source_target_pairs={{0,2},{1,3},{2,0},{3,1},{4,6},{5,7},{6,4},{7,5},{8,10},{9,11},{10,... | collective-permute-start | bytes 3145736 | tf_op jit(solution)/shard_map/ppermute | solution.py:380
  3.8 70.1 %collective-permute-start.1 = (s32[2,256]{1,0:T(2,128)S(1)}, s32[2,256]{1,0:T(2,128)S(1)}, u32[]{:S(2)}, u32[]{:S(2)}) collective-permute-start(s32[2,256]{1,0:T(2,128)S(1)} %get-tuple-element.97), channel_id=1, source_target_pairs={{0,2},{1,3},{2,0},{3,1},{4,6},{5,7},{6,4},{7,5},{8,10},{9,11},{10,... | collective-permute-start | bytes 6152 | tf_op jit(solution)/shard_map/ppermute | solution.py:374
  33.1 63.6 %collective-permute-start.8 = (bf16[256,4096]{1,0:T(8,128)(2,1)}, bf16[256,4096]{1,0:T(8,128)(2,1)}, u32[]{:S(2)}, u32[]{:S(2)}) collective-permute-start(bf16[256,4096]{1,0:T(8,128)(2,1)} %get-tuple-element.47.refs_0_), channel_id=1, source_target_pairs={{0,1},{1,0},{2,3},{3,2},{4,5},{5,4},{6,7},{7,6},{8,9},{9,8},{10,11... | collective-permute-start | bytes 6291464 | tf_op jit(solution)/shard_map/ppermute | solution.py:414
  54.0 31.7 %collective-permute-start.5 = (bf16[256,4096]{1,0:T(8,128)(2,1)}, bf16[256,4096]{1,0:T(8,128)(2,1)}, u32[]{:S(2)}, u32[]{:S(2)}) collective-permute-start(bf16[256,4096]{1,0:T(8,128)(2,1)} %get-tuple-element.44.refs_0_), channel_id=1, source_target_pairs={{0,1},{1,0},{2,3},{3,2},{4,5},{5,4},{6,7},{7,6},{8,9},{9,8},{10,11... | collective-permute-start | bytes 6291464 | tf_op jit(solution)/shard_map/ppermute | solution.py:414
  74.0 1.4 collective-permute-start.2
  77.5 3.6 collective-permute-start.3
  81.2 4.5 collective-permute-start.4
  93.1 24.4 %collective-permute-start.6 = (bf16[512,512]{1,0:T(8,128)(2,1)S(1)}, bf16[512,512]{1,0:T(8,128)(2,1)S(1)}, u32[]{:S(2)}, u32[]{:S(2)}) collective-permute-start(bf16[512,512]{1,0:T(8,128)(2,1)S(1)} %shard_map.119.refs_2_.refs_6_), channel_id=1, source_target_pairs={{0,4},{4,8},{8,12},{1,5},{5,9},{9,13},{2,6},{6,10},{10,14},{3,7},{... | collective-permute-start | bytes 1572872 | tf_op jit(solution)/shard_map/ppermute | solution.py:439
  101.7 16.4 %collective-permute-start.9 = (bf16[512,512]{1,0:T(8,128)(2,1)S(1)}, bf16[512,512]{1,0:T(8,128)(2,1)S(1)}, u32[]{:S(2)}, u32[]{:S(2)}) collective-permute-start(bf16[512,512]{1,0:T(8,128)(2,1)S(1)} %shard_map.120.refs_4_.refs_8_), channel_id=1, source_target_pairs={{0,4},{4,8},{8,12},{1,5},{5,9},{9,13},{2,6},{6,10},{10,14},{3,7},{... | collective-permute-start | bytes 1572872 | tf_op jit(solution)/shard_map/ppermute | solution.py:439
  137.3 29.9 %collective-permute-start.10 = (bf16[256,4096]{1,0:T(8,128)(2,1)S(1)}, bf16[256,4096]{1,0:T(8,128)(2,1)}, u32[]{:S(2)}, u32[]{:S(2)}) collective-permute-start(bf16[256,4096]{1,0:T(8,128)(2,1)S(1)} %get-tuple-element.49), channel_id=1, source_target_pairs={{0,1},{1,0},{2,3},{3,2},{4,5},{5,4},{6,7},{7,6},{8,9},{9,8},{10,11... | collective-permute-start | bytes 6291464 | tf_op jit(solution)/shard_map/ppermute | solution.py:417
  166.6 4.6 collective-permute-start.19
  169.6 48.6 %collective-permute-start.11 = (bf16[256,4096]{1,0:T(8,128)(2,1)S(1)}, bf16[256,4096]{1,0:T(8,128)(2,1)S(1)}, u32[]{:S(2)}, u32[]{:S(2)}) collective-permute-start(bf16[256,4096]{1,0:T(8,128)(2,1)S(1)} %add_convert_fusion.7.s_ref), channel_id=1, source_target_pairs={{0,2},{1,3},{2,0},{3,1},{4,6},{5,7},{6,4},{7,5},{8,10},{9,11},{10,... | collective-permute-start | bytes 6291464 | tf_op jit(solution)/shard_map/ppermute | solution.py:419
  172.0 90.2 %collective-permute-start.20 = (bf16[256,4096]{1,0:T(8,128)(2,1)S(1)}, bf16[256,4096]{1,0:T(8,128)(2,1)S(1)}, u32[]{:S(2)}, u32[]{:S(2)}) collective-permute-start(bf16[256,4096]{1,0:T(8,128)(2,1)S(1)} %add_convert_fusion.5.s_ref), channel_id=1, source_target_pairs={{0,2},{1,3},{2,0},{3,1},{4,6},{5,7},{6,4},{7,5},{8,10},{9,11},{10,... | collective-permute-start | bytes 6291464 | tf_op jit(solution)/shard_map/ppermute | solution.py:419
  219.8 44.0 %copy-start.7 = (bf16[256,4096]{1,0:T(8,128)(2,1)}, bf16[256,4096]{1,0:T(8,128)(2,1)S(1)}, u32[]{:S(2)}) copy-start(bf16[256,4096]{1,0:T(8,128)(2,1)S(1)} %get-tuple-element.51.refs_0_) | copy-start | bytes 6291460
  219.9 45.3 %collective-permute-start.12 = (bf16[256,4096]{1,0:T(8,128)(2,1)S(1)}, bf16[256,4096]{1,0:T(8,128)(2,1)}, u32[]{:S(2)}, u32[]{:S(2)}) collective-permute-start(bf16[256,4096]{1,0:T(8,128)(2,1)S(1)} %get-tuple-element.51.refs_0_), channel_id=1, source_target_pairs={{0,1},{1,0},{2,3},{3,2},{4,5},{5,4},{6,7},{7,6},{8,9},{9,8},{10,11... | collective-permute-start | bytes 6291464 | tf_op jit(solution)/shard_map/ppermute | solution.py:414
  265.2 58.3 %copy-start.9 = (bf16[256,4096]{1,0:T(8,128)(2,1)}, bf16[256,4096]{1,0:T(8,128)(2,1)S(1)}, u32[]{:S(2)}) copy-start(bf16[256,4096]{1,0:T(8,128)(2,1)S(1)} %get-tuple-element.62.refs_0_) | copy-start | bytes 6291460
  265.2 58.7 %collective-permute-start.21 = (bf16[256,4096]{1,0:T(8,128)(2,1)S(1)}, bf16[256,4096]{1,0:T(8,128)(2,1)}, u32[]{:S(2)}, u32[]{:S(2)}) collective-permute-start(bf16[256,4096]{1,0:T(8,128)(2,1)S(1)} %get-tuple-element.62.refs_0_), channel_id=1, source_target_pairs={{0,1},{1,0},{2,3},{3,2},{4,5},{5,4},{6,7},{7,6},{8,9},{9,8},{10,11... | collective-permute-start | bytes 6291464 | tf_op jit(solution)/shard_map/ppermute | solution.py:414
  323.5 58.5 %copy-start.33 = (bf16[256,4096]{1,0:T(8,128)(2,1)S(1)}, bf16[256,4096]{1,0:T(8,128)(2,1)}, u32[]{:S(2)}) copy-start(bf16[256,4096]{1,0:T(8,128)(2,1)} %get-tuple-element.52) | copy-start | bytes 6291460
  323.5 58.4 %collective-permute-start.13 = (bf16[256,4096]{1,0:T(8,128)(2,1)}, bf16[256,4096]{1,0:T(8,128)(2,1)}, u32[]{:S(2)}, u32[]{:S(2)}) collective-permute-start(bf16[256,4096]{1,0:T(8,128)(2,1)} %get-tuple-element.53), channel_id=1, source_target_pairs={{0,1},{1,0},{2,3},{3,2},{4,5},{5,4},{6,7},{7,6},{8,9},{9,8},{10,11... | collective-permute-start | bytes 6291464 | tf_op jit(solution)/shard_map/ppermute | solution.py:417
  381.7 4.4 collective-permute-start.22
  384.5 48.6 %collective-permute-start.14 = (bf16[256,4096]{1,0:T(8,128)(2,1)S(1)}, bf16[256,4096]{1,0:T(8,128)(2,1)S(1)}, u32[]{:S(2)}, u32[]{:S(2)}) collective-permute-start(bf16[256,4096]{1,0:T(8,128)(2,1)S(1)} %add_convert_fusion.6.s_ref), channel_id=1, source_target_pairs={{0,2},{1,3},{2,0},{3,1},{4,6},{5,7},{6,4},{7,5},{8,10},{9,11},{10,... | collective-permute-start | bytes 6291464 | tf_op jit(solution)/shard_map/ppermute | solution.py:419
  386.1 46.9 %copy-start.16 = (bf16[256,4096]{1,0:T(8,128)(2,1)S(1)}, bf16[256,4096]{1,0:T(8,128)(2,1)}, u32[]{:S(2)}) copy-start(bf16[256,4096]{1,0:T(8,128)(2,1)} %copy-done.15) | copy-start | bytes 6291460
  386.9 90.4 %collective-permute-start.23 = (bf16[256,4096]{1,0:T(8,128)(2,1)S(1)}, bf16[256,4096]{1,0:T(8,128)(2,1)S(1)}, u32[]{:S(2)}, u32[]{:S(2)}) collective-permute-start(bf16[256,4096]{1,0:T(8,128)(2,1)S(1)} %add_convert_fusion.4.s_ref), channel_id=1, source_target_pairs={{0,2},{1,3},{2,0},{3,1},{4,6},{5,7},{6,4},{7,5},{8,10},{9,11},{10,... | collective-permute-start | bytes 6291464 | tf_op jit(solution)/shard_map/ppermute | solution.py:419
  433.0 44.3 %copy-start.14 = (bf16[256,4096]{1,0:T(8,128)(2,1)S(1)}, bf16[256,4096]{1,0:T(8,128)(2,1)}, u32[]{:S(2)}) copy-start(bf16[256,4096]{1,0:T(8,128)(2,1)} %copy-done.13) | copy-start | bytes 6291460
  435.9 61.2 %collective-permute-start.15 = (bf16[256,4096]{1,0:T(8,128)(2,1)}, bf16[256,4096]{1,0:T(8,128)(2,1)}, u32[]{:S(2)}, u32[]{:S(2)}) collective-permute-start(bf16[256,4096]{1,0:T(8,128)(2,1)} %get-tuple-element.55.refs_0_), channel_id=1, source_target_pairs={{0,1},{1,0},{2,3},{3,2},{4,5},{5,4},{6,7},{7,6},{8,9},{9,8},{10,11... | collective-permute-start | bytes 6291464 | tf_op jit(solution)/shard_map/ppermute | solution.py:414
  479.0 28.3 %collective-permute-start.24 = (bf16[256,4096]{1,0:T(8,128)(2,1)S(1)}, bf16[256,4096]{1,0:T(8,128)(2,1)S(1)}, u32[]{:S(2)}, u32[]{:S(2)}) collective-permute-start(bf16[256,4096]{1,0:T(8,128)(2,1)S(1)} %get-tuple-element.65.refs_0_), channel_id=1, source_target_pairs={{0,1},{1,0},{2,3},{3,2},{4,5},{5,4},{6,7},{7,6},{8,9},{9,8},{10,11... | collective-permute-start | bytes 6291464 | tf_op jit(solution)/shard_map/ppermute | solution.py:414
  502.2 86.0 %collective-permute-start.16 = (bf16[512,512]{1,0:T(8,128)(2,1)S(1)}, bf16[512,512]{1,0:T(8,128)(2,1)S(1)}, u32[]{:S(2)}, u32[]{:S(2)}) collective-permute-start(bf16[512,512]{1,0:T(8,128)(2,1)S(1)} %shard_map.122.refs_2_), channel_id=1, source_target_pairs={{0,4},{4,8},{8,12},{1,5},{5,9},{9,13},{2,6},{6,10},{10,14},{3,7},{... | collective-permute-start | bytes 1572872 | tf_op jit(solution)/shard_map/ppermute | solution.py:439
  504.5 84.4 %collective-permute-start.17 = (bf16[512,512]{1,0:T(8,128)(2,1)S(1)}, bf16[512,512]{1,0:T(8,128)(2,1)S(1)}, u32[]{:S(2)}, u32[]{:S(2)}) collective-permute-start(bf16[512,512]{1,0:T(8,128)(2,1)S(1)} %shard_map.122.refs_2_), channel_id=1, source_target_pairs={{0,8},{4,12},{1,9},{5,13},{2,10},{6,14},{3,11},{7,15},{16,24},{20,... | collective-permute-start | bytes 1572872 | tf_op jit(solution)/shard_map/ppermute | solution.py:439
  505.9 83.0 %collective-permute-start.18 = (bf16[512,512]{1,0:T(8,128)(2,1)S(1)}, bf16[512,512]{1,0:T(8,128)(2,1)}, u32[]{:S(2)}, u32[]{:S(2)}) collective-permute-start(bf16[512,512]{1,0:T(8,128)(2,1)S(1)} %shard_map.122.refs_2_), channel_id=1, source_target_pairs={{0,12},{1,13},{2,14},{3,15},{16,28},{17,29},{18,30},{19,31}} | collective-permute-start | bytes 1572872 | tf_op jit(solution)/shard_map/ppermute | solution.py:439
  511.1 63.8 %collective-permute-start.25 = (bf16[512,256]{1,0:T(8,128)(2,1)}, bf16[512,256]{1,0:T(8,128)(2,1)S(1)}, u32[]{:S(2)}, u32[]{:S(2)}) collective-permute-start(bf16[512,256]{1,0:T(8,128)(2,1)} %get-tuple-element.66.refs_6_), channel_id=1, source_target_pairs={{0,4},{4,8},{8,12},{1,5},{5,9},{9,13},{2,6},{6,10},{10,14},{3,7},{... | collective-permute-start | bytes 786440 | tf_op jit(solution)/shard_map/ppermute | solution.py:439
  513.1 71.9 %collective-permute-start.26 = (bf16[512,256]{1,0:T(8,128)(2,1)}, bf16[512,256]{1,0:T(8,128)(2,1)}, u32[]{:S(2)}, u32[]{:S(2)}) collective-permute-start(bf16[512,256]{1,0:T(8,128)(2,1)} %get-tuple-element.66.refs_6_), channel_id=1, source_target_pairs={{0,8},{4,12},{1,9},{5,13},{2,10},{6,14},{3,11},{7,15},{16,24},{20,... | collective-permute-start | bytes 786440 | tf_op jit(solution)/shard_map/ppermute | solution.py:439
  575.6 11.3 %collective-permute-start.27 = (bf16[512,256]{1,0:T(8,128)(2,1)}, bf16[512,256]{1,0:T(8,128)(2,1)S(1)}, u32[]{:S(2)}, u32[]{:S(2)}) collective-permute-start(bf16[512,256]{1,0:T(8,128)(2,1)} %get-tuple-element.66.refs_6_), channel_id=1, source_target_pairs={{0,12},{1,13},{2,14},{3,15},{16,28},{17,29},{18,30},{19,31}} | collective-permute-start | bytes 786440 | tf_op jit(solution)/shard_map/ppermute | solution.py:439
  585.0 22.3 %collective-permute-start.28 = (bf16[512,256]{1,0:T(8,128)(2,1)S(1)}, bf16[512,256]{1,0:T(8,128)(2,1)S(1)}, u32[]{:S(2)}, u32[]{:S(2)}) collective-permute-start(bf16[512,256]{1,0:T(8,128)(2,1)S(1)} %get-tuple-element.67.refs_6_), channel_id=1, source_target_pairs={{0,4},{4,8},{8,12},{1,5},{5,9},{9,13},{2,6},{6,10},{10,14},{3,7},{... | collective-permute-start | bytes 786440 | tf_op jit(solution)/shard_map/ppermute | solution.py:439
  586.9 20.4 %collective-permute-start.29 = (bf16[512,256]{1,0:T(8,128)(2,1)S(1)}, bf16[512,256]{1,0:T(8,128)(2,1)S(1)}, u32[]{:S(2)}, u32[]{:S(2)}) collective-permute-start(bf16[512,256]{1,0:T(8,128)(2,1)S(1)} %get-tuple-element.67.refs_6_), channel_id=1, source_target_pairs={{0,8},{4,12},{1,9},{5,13},{2,10},{6,14},{3,11},{7,15},{16,24},{20,... | collective-permute-start | bytes 786440 | tf_op jit(solution)/shard_map/ppermute | solution.py:439
  588.2 19.1 %collective-permute-start.30 = (bf16[512,256]{1,0:T(8,128)(2,1)S(1)}, bf16[512,256]{1,0:T(8,128)(2,1)S(1)}, u32[]{:S(2)}, u32[]{:S(2)}) collective-permute-start(bf16[512,256]{1,0:T(8,128)(2,1)S(1)} %get-tuple-element.67.refs_6_), channel_id=1, source_target_pairs={{0,12},{1,13},{2,14},{3,15},{16,28},{17,29},{18,30},{19,31}} | collective-permute-start | bytes 786440 | tf_op jit(solution)/shard_map/ppermute | solution.py:439
  625.6 33.6 %collective-permute-start.36 = (bf16[256,4096]{1,0:T(8,128)(2,1)S(1)}, bf16[256,4096]{1,0:T(8,128)(2,1)S(1)}, u32[]{:S(2)}, u32[]{:S(2)}) collective-permute-start(bf16[256,4096]{1,0:T(8,128)(2,1)S(1)} %get-tuple-element.76), channel_id=1, source_target_pairs={{0,1},{1,0},{2,3},{3,2},{4,5},{5,4},{6,7},{7,6},{8,9},{9,8},{10,11... | collective-permute-start | bytes 6291464 | tf_op jit(solution)/shard_map/ppermute | solution.py:417
  658.6 4.3 collective-permute-start.31
  659.9 48.6 %collective-permute-start.37 = (bf16[256,4096]{1,0:T(8,128)(2,1)S(1)}, bf16[256,4096]{1,0:T(8,128)(2,1)S(1)}, u32[]{:S(2)}, u32[]{:S(2)}) collective-permute-start(bf16[256,4096]{1,0:T(8,128)(2,1)S(1)} %add_convert_fusion.1.s_ref), channel_id=1, source_target_pairs={{0,2},{1,3},{2,0},{3,1},{4,6},{5,7},{6,4},{7,5},{8,10},{9,11},{10,... | collective-permute-start | bytes 6291464 | tf_op jit(solution)/shard_map/ppermute | solution.py:419
  663.7 88.8 %collective-permute-start.32 = (bf16[256,4096]{1,0:T(8,128)(2,1)S(1)}, bf16[256,4096]{1,0:T(8,128)(2,1)S(1)}, u32[]{:S(2)}, u32[]{:S(2)}) collective-permute-start(bf16[256,4096]{1,0:T(8,128)(2,1)S(1)} %add_convert_fusion.3.s_ref), channel_id=1, source_target_pairs={{0,2},{1,3},{2,0},{3,1},{4,6},{5,7},{6,4},{7,5},{8,10},{9,11},{10,... | collective-permute-start | bytes 6291464 | tf_op jit(solution)/shard_map/ppermute | solution.py:419
  710.2 45.3 %collective-permute-start.38 = (bf16[256,4096]{1,0:T(8,128)(2,1)S(1)}, bf16[256,4096]{1,0:T(8,128)(2,1)}, u32[]{:S(2)}, u32[]{:S(2)}) collective-permute-start(bf16[256,4096]{1,0:T(8,128)(2,1)S(1)} %get-tuple-element.78.refs_0_), channel_id=1, source_target_pairs={{0,1},{1,0},{2,3},{3,2},{4,5},{5,4},{6,7},{7,6},{8,9},{9,8},{10,11... | collective-permute-start | bytes 6291464 | tf_op jit(solution)/shard_map/ppermute | solution.py:414
  755.5 58.3 %copy-start.10 = (bf16[256,4096]{1,0:T(8,128)(2,1)}, bf16[256,4096]{1,0:T(8,128)(2,1)S(1)}, u32[]{:S(2)}) copy-start(bf16[256,4096]{1,0:T(8,128)(2,1)S(1)} %get-tuple-element.71.refs_0_) | copy-start | bytes 6291460
  755.5 58.4 %collective-permute-start.33 = (bf16[256,4096]{1,0:T(8,128)(2,1)S(1)}, bf16[256,4096]{1,0:T(8,128)(2,1)}, u32[]{:S(2)}, u32[]{:S(2)}) collective-permute-start(bf16[256,4096]{1,0:T(8,128)(2,1)S(1)} %get-tuple-element.71.refs_0_), channel_id=1, source_target_pairs={{0,1},{1,0},{2,3},{3,2},{4,5},{5,4},{6,7},{7,6},{8,9},{9,8},{10,11... | collective-permute-start | bytes 6291464 | tf_op jit(solution)/shard_map/ppermute | solution.py:414
  813.9 58.6 %copy-start.35 = (bf16[256,4096]{1,0:T(8,128)(2,1)S(1)}, bf16[256,4096]{1,0:T(8,128)(2,1)}, u32[]{:S(2)}) copy-start(bf16[256,4096]{1,0:T(8,128)(2,1)} %get-tuple-element.79) | copy-start | bytes 6291460
  813.9 58.6 %collective-permute-start.39 = (bf16[256,4096]{1,0:T(8,128)(2,1)}, bf16[256,4096]{1,0:T(8,128)(2,1)}, u32[]{:S(2)}, u32[]{:S(2)}) collective-permute-start(bf16[256,4096]{1,0:T(8,128)(2,1)} %get-tuple-element.80), channel_id=1, source_target_pairs={{0,1},{1,0},{2,3},{3,2},{4,5},{5,4},{6,7},{7,6},{8,9},{9,8},{10,11... | collective-permute-start | bytes 6291464 | tf_op jit(solution)/shard_map/ppermute | solution.py:422
  872.0 4.6 collective-permute-start.34
  874.9 26.1 %collective-permute-start.40 = (bf16[128,4096]{1,0:T(8,128)(2,1)S(1)}, bf16[128,4096]{1,0:T(8,128)(2,1)S(1)}, u32[]{:S(2)}, u32[]{:S(2)}) collective-permute-start(bf16[128,4096]{1,0:T(8,128)(2,1)S(1)} %slice.84), channel_id=1, source_target_pairs={{0,2},{1,3},{2,0},{3,1},{4,6},{5,7},{6,4},{7,5},{8,10},{9,11},{10,... | collective-permute-start | bytes 3145736 | tf_op jit(solution)/shard_map/ppermute | solution.py:424
  877.4 45.2 %collective-permute-start.35 = (bf16[128,4096]{1,0:T(8,128)(2,1)S(1)}, bf16[128,4096]{1,0:T(8,128)(2,1)S(1)}, u32[]{:S(2)}, u32[]{:S(2)}) collective-permute-start(bf16[128,4096]{1,0:T(8,128)(2,1)S(1)} %slice.82), channel_id=1, source_target_pairs={{0,2},{1,3},{2,0},{3,1},{4,6},{5,7},{6,4},{7,5},{8,10},{9,11},{10,... | collective-permute-start | bytes 3145736 | tf_op jit(solution)/shard_map/ppermute | solution.py:424
  (33 other events, 397.0 us)
